TPU v7x, 256 devices: a 4x2x16 block of a 4x16x16 slice. The times are simulated.
256 devices in a mesh: grp: 2 (over y), blk: 16 (over z), node: 4 (over x), pair: 2 (over core).
Axes of the slice: x: 4, y: 2, z: 16, core: 2. Of those that a mesh axis runs over, the one named last changes fastest.
The devices are a block of a 4x16x16 slice.
Arguments:
- query: bfloat16 [18432, 1280], P(('grp', 'blk', 'node'), 'pair'), parts along dimension 0, may hold values from -600 to 600
- key: bfloat16 [18432, 1280], P(('grp', 'blk', 'node'), 'pair'), parts along dimension 0, may hold values from -25 to 25
- value: bfloat16 [18432, 1280], P(('grp', 'blk', 'node'), 'pair'), parts along dimension 0, may hold values from -6 to 6
- out_weight: bfloat16 [1280, 1280], P('pair'), may hold values from -0.15625 to 0.15625
Outputs:
- mixed: bfloat16 [18432, 1280], P(('grp', 'blk', 'node', 'pair')), parts along dimension 0
There are 2 independent parts, one for each index of `grp`. A program takes and returns all parts, laid end to end along the dimension named above; an argument that names none is the same for every part. Nothing has to cross between parts.
All inputs are finite; a program needn't handle non-finite values.
Results may differ from a plain program's by a relative error of at most 0.011.
Values may be sent and summed in bfloat16 or wider, within the bound.
No kernel may reach another device: no remote copies, remote signals or barrier semaphores. Data moves between devices by JAX's collectives and lax.ppermute only.
A program may use at most 128 MiB of HBM per device.

v0:
```python
import math

import jax
import jax.numpy as jnp
from jax import lax
from jax.experimental import pallas as pl
from jax.experimental.pallas import tpu as pltpu
from jax.sharding import PartitionSpec as P


HD = 64
LANES = 128


def round_up(value, unit):
    return -(-value // unit) * unit


def shifted(array, axis, by):
    size = lax.axis_size(axis)
    return lax.ppermute(array, axis, [(i, (i + by) % size) for i in range(size)])


def split_three(x):
    hi = x.astype(jnp.bfloat16).astype(jnp.float32)
    rest = x - hi
    mid = rest.astype(jnp.bfloat16).astype(jnp.float32)
    return hi, mid, rest - mid


def attend_step(queries, pieces, state, last, blocks=None):
    count, features = queries.shape
    pairs = features // LANES
    heads = features // HD
    hrows = round_up(heads + 1, 8)
    factor = (1.0 / math.sqrt(HD)) * math.log2(math.e)
    fresh_state = state is None

    args = [queries]
    spots = []
    for k, k_at, v, v_at, size in pieces:
        args.append(k)
        at = len(args) - 1
        if v is not k:
            args.append(v)
        spots.append((at, slice(k_at, k_at + size), len(args) - 1, slice(v_at, v_at + size)))
    first = len(args)
    if not fresh_state:
        args += list(state)
    inputs = len(args)
    rows = sum(p[4] for p in pieces)
    outputs = 3 if not last else 2 + len(blocks)

    def body(*refs):
        q_ref = refs[0]
        if not fresh_state:
            m_in, l_in, a_in = refs[first : first + 3]
        outs = refs[inputs : inputs + outputs]
        m_out, l_out = outs[:2]
        s0_ref, s1_ref, p0_ref, p1_ref, vt_ref, fade_ref = refs[inputs + outputs :][:6]
        a_out = refs[-1] if last else outs[2]

        def lanes_of(p):
            return pl.ds(pl.multiple_of(p * LANES, LANES), LANES)

        def score(p, side):
            kk = jnp.concatenate([refs[i][at, lanes_of(p)] for i, at, _, _ in spots], axis=0)
            qq = q_ref[:, lanes_of(p)]
            lane = lax.broadcasted_iota(jnp.int32, qq.shape, 1)
            mine = (lane < HD) if side == 0 else (lane >= HD)
            qm = jnp.where(mine, qq, jnp.zeros_like(qq))
            return lax.dot_general(
                kk, qm, (((1,), (1,)), ((), ())), preferred_element_type=jnp.float32
            )

        def softmax(h, s_ref, p_ref):
            row = pl.ds(h, 1)
            peak = s_ref[0:8, :]
            for at in range(8, rows, 8):
                peak = jnp.maximum(peak, s_ref[at : at + 8, :])
            peak = jnp.max(peak, axis=0, keepdims=True)
            if not fresh_state:
                old = m_in[row, :]
                peak = jnp.maximum(old, peak)
                fade_ref[row, :] = jnp.exp2((old - peak) * factor)
            m_out[row, :] = peak
            for at in range(0, rows, 16):
                part = s_ref[at : at + 16, :]
                p_ref[at : at + 16, :] = jnp.exp2((part - peak) * factor).astype(jnp.bfloat16)

        def values(h, expo, vt):
            vs = jnp.concatenate([vt, jnp.ones((16, rows), vt.dtype)], axis=0)
            pv = jnp.dot(vs, expo, preferred_element_type=jnp.float32)
            acc = pv[:HD, :]
            total = pv[HD : HD + 1, :]
            row = pl.ds(h, 1)
            arows = pl.ds(pl.multiple_of(h * HD, HD), HD)
            if not fresh_state:
                fade = fade_ref[row, :]
                acc = a_in[arows, :] * fade + acc
                total = l_in[row, :] * fade + total
            l_out[row, :] = total
            a_out[arows, :] = acc / total if last else acc

        def pair_step(p, carry):
            h = 2 * p
            vv = jnp.concatenate([refs[i][at, lanes_of(p)] for _, _, i, at in spots], axis=0)
            vt = vv.T
            s1_ref[...] = score(p, 1)
            softmax(h, s0_ref, p0_ref)
            values(jnp.where(p == 0, heads, h - 1), p1_ref[...], vt_ref[...])
            s0_ref[...] = score(jnp.minimum(p + 1, pairs - 1), 0)
            softmax(h + 1, s1_ref, p1_ref)
            values(h, p0_ref[...], vt[:HD, :])
            vt_ref[...] = vt[HD:, :]
            return carry

        s0_ref[...] = score(0, 0)
        lax.fori_loop(0, pairs, pair_step, 0)
        values(heads - 1, p1_ref[...], vt_ref[...])
        if last:
            dead = lax.broadcasted_iota(jnp.int32, m_out.shape, 0) >= heads
            m_out[...] = jnp.where(dead, 1.0, m_out[...])
            l_out[...] = jnp.where(dead, 1.0, l_out[...])

            def write(lanes, array):
                at = 0
                for o_ref, size in zip(outs[2:], blocks):
                    o_ref[:, lanes] = array[at : at + size, :]
                    at += size

            for p in range(pairs):
                lanes = slice(p * LANES, (p + 1) * LANES)
                write(lanes, a_out[lanes, :].T.astype(jnp.bfloat16))
            parts = [*split_three(m_out[...]), *split_three(l_out[...])]
            parts.append(jnp.zeros((LANES - 6 * hrows, count), jnp.float32))
            stats = jnp.concatenate(parts, axis=0).T.astype(jnp.bfloat16)
            write(slice(features, features + LANES), stats)

    stat = jax.ShapeDtypeStruct((hrows, count), jnp.float32)
    aliases = {}
    if last:
        wide = features + LANES
        outs = (stat, stat) + tuple(jax.ShapeDtypeStruct((n, wide), jnp.bfloat16) for n in blocks)
    else:
        outs = (stat, stat, jax.ShapeDtypeStruct((features + HD, count), jnp.float32))
        if not fresh_state:
            aliases = {first: 0, first + 1: 1, first + 2: 2}
    scratch = [
        pltpu.VMEM((rows, count), jnp.float32),
        pltpu.VMEM((rows, count), jnp.float32),
        pltpu.VMEM((rows, count), jnp.bfloat16),
        pltpu.VMEM((rows, count), jnp.bfloat16),
        pltpu.VMEM((HD, rows), jnp.bfloat16),
        pltpu.VMEM((hrows, count), jnp.float32),
    ]
    if last:
        scratch.append(pltpu.VMEM((features + HD, count), jnp.float32))
    vmem = pl.BlockSpec(memory_space=pltpu.VMEM)
    return pl.pallas_call(
        body,
        out_shape=outs,
        in_specs=[vmem] * inputs,
        out_specs=tuple([vmem] * outputs),
        input_output_aliases=aliases,
        scratch_shapes=scratch,
        cost_estimate=pl.CostEstimate(
            flops=4 * rows * count * features,
            transcendentals=rows * count * heads,
            bytes_accessed=4 * count * features,
        ),
        compiler_params=pltpu.CompilerParams(vmem_limit_bytes=16 * 2**20),
        name="attend",
    )(*args)


def merge_project(parts, weight):
    items, wide = parts[0].shape
    features = wide - LANES
    heads = features // HD
    hrows = round_up(heads + 1, 8)
    width = weight.shape[1]
    factor = (1.0 / math.sqrt(HD)) * math.log2(math.e)

    def body(*refs):
        w_ref, o_ref = refs[-2], refs[-1]
        stats = [r[:, features:].astype(jnp.float32) for r in refs[:-2]]

        def stat(x, which):
            at = 3 * which * hrows
            return (
                x[:, at : at + hrows]
                + x[:, at + hrows : at + 2 * hrows]
                + x[:, at + 2 * hrows : at + 3 * hrows]
            )

        peaks = [stat(x, 0) for x in stats]
        best = peaks[0]
        for m in peaks[1:]:
            best = jnp.maximum(best, m)
        shares = [jnp.exp2((m - best) * factor) * stat(x, 1) for m, x in zip(peaks, stats)]
        total = shares[0]
        for w in shares[1:]:
            total = total + w
        shares = [w / total for w in shares]
        lane = lax.broadcasted_iota(jnp.int32, (items, LANES), 1)
        columns = []
        for p in range(features // LANES):
            joined = jnp.zeros((items, LANES), jnp.float32)
            for r, w in zip(refs[:-2], shares):
                scale = jnp.where(lane < HD, w[:, 2 * p : 2 * p + 1], w[:, 2 * p + 1 : 2 * p + 2])
                joined += r[:, p * LANES : (p + 1) * LANES].astype(jnp.float32) * scale
            columns.append(joined.astype(jnp.bfloat16))
        attn = jnp.concatenate(columns, axis=1)
        out = jnp.dot(attn, w_ref[...], preferred_element_type=jnp.float32)
        o_ref[...] = out.astype(jnp.bfloat16)

    vmem = pl.BlockSpec(memory_space=pltpu.VMEM)
    return pl.pallas_call(
        body,
        out_shape=jax.ShapeDtypeStruct((items, width), jnp.bfloat16),
        in_specs=[vmem] * (len(parts) + 1),
        out_specs=vmem,
        cost_estimate=pl.CostEstimate(
            flops=2 * items * features * width,
            transcendentals=0,
            bytes_accessed=2 * features * width,
        ),
        compiler_params=pltpu.CompilerParams(vmem_limit_bytes=16 * 2**20),
        name="merge_project",
    )(*parts, weight)


def per_device(query, key, value, out_weight):
    rows, features = query.shape
    blks = lax.axis_size("blk")
    nodes = lax.axis_size("node")
    half = blks // 2

    def piece(both):
        return (both, 0, both, rows, rows)

    own = jnp.concatenate([key, value], axis=0)
    up = down = own
    held = [piece(own)]
    state = None
    for turn in range(1, half + 1):
        final = turn == half
        if final:
            k = shifted(up[:rows], "blk", 1)
            v = shifted(down[rows:], "blk", -1)
            arrived = [(k, 0, v, 0, rows)]
        else:
            up = shifted(up, "blk", 1)
            down = shifted(down, "blk", -1)
            arrived = [piece(up), piece(down)]
        if turn == 1:
            stack = [query] + [shifted(query, "node", d) for d in range(1, nodes)]
            blocks = [rows] * nodes
            padded = round_up(rows * nodes, LANES)
            if padded > rows * nodes:
                stack.append(jnp.zeros((padded - rows * nodes, features), query.dtype))
            queries = jnp.concatenate(stack, axis=0)
        else:
            state = attend_step(queries, held, state, False)
            held = []
        held = held + arrived

    parts = list(attend_step(queries, held, state, True, blocks)[2:])
    for d in range(1, nodes):
        parts[d] = shifted(parts[d], "node", -d)
    mine = merge_project(parts, out_weight)

    cores = lax.axis_size("pair")
    at = lax.axis_index("pair")
    tiles = mine.reshape(cores, rows // cores, mine.shape[1])
    summed = lax.dynamic_index_in_dim(tiles, at, 0, keepdims=False).astype(jnp.float32)
    for d in range(1, cores):
        away = lax.dynamic_index_in_dim(tiles, (at + d) % cores, 0, keepdims=False)
        summed = summed + shifted(away, "pair", d).astype(jnp.float32)
    return summed.astype(jnp.bfloat16)


def solution(mesh):
    in_specs = (
        P(("grp", "blk", "node"), "pair"),
        P(("grp", "blk", "node"), "pair"),
        P(("grp", "blk", "node"), "pair"),
        P("pair", None),
    )
    out_specs = P(("grp", "blk", "node", "pair"), None)

    return jax.shard_map(
        per_device, mesh=mesh, in_specs=in_specs, out_specs=out_specs, check_vma=False
    )
```

profile of v0, /device:TPU:33, one launch (start us, length us, event | category | flops | bytes accessed | tf_op | source)
XLA Modules:
  0.0 142.2 jit_solution(16967253111497021471)
XLA Ops:
  1.9 23.0 %collective-permute-start.11 = (bf16[288,640]{1,0:T(8,128)(2,1)S(1)}, bf16[288,640]{1,0:T(8,128)(2,1)S(1)}, u32[]{:S(2)}, u32[]{:S(2)}) collective-permute-start(bf16[288,640]{1,0:T(8,128)(2,1)S(1)} %constant_dynamic-update-slice_fusion.4.refs_1_), channel_id=1, source_target_pairs={{0,120},{8,0},{16,8},{24,16},{32,24},{40,32},{48,40},{56,48},{64,5... | collective-permute-start | bytes 1105928 | tf_op jit(solution)/shard_map/ppermute | solution.py:21
  24.9 7.3 %collective-permute-done.11.refs_3_ = bf16[288,640]{1,0:T(8,128)(2,1)S(1)} collective-permute-done((bf16[288,640]{1,0:T(8,128)(2,1)S(1)}, bf16[288,640]{1,0:T(8,128)(2,1)S(1)}, u32[]{:S(2)}, u32[]{:S(2)}) %collective-permute-start.11) | collective-permute-done | bytes 368672 | tf_op jit(solution)/shard_map/ppermute | solution.py:21
  32.3 3.4 %collective-permute-start.12 = (bf16[288,640]{1,0:T(8,128)(2,1)S(1)}, bf16[288,640]{1,0:T(8,128)(2,1)S(1)}, u32[]{:S(2)}, u32[]{:S(2)}) collective-permute-start(bf16[288,640]{1,0:T(8,128)(2,1)S(1)} %collective-permute-done.11.refs_3_), channel_id=1, source_target_pairs={{0,120},{8,0},{16,8},{24,16},{32,24},{40,32},{48,40},{56,48},{64,5... | collective-permute-start | bytes 1105928 | tf_op jit(solution)/shard_map/ppermute | solution.py:21
  35.7 6.5 %collective-permute-done.12.refs_2_ = bf16[288,640]{1,0:T(8,128)(2,1)S(1)} collective-permute-done((bf16[288,640]{1,0:T(8,128)(2,1)S(1)}, bf16[288,640]{1,0:T(8,128)(2,1)S(1)}, u32[]{:S(2)}, u32[]{:S(2)}) %collective-permute-start.12) | collective-permute-done | bytes 368672 | tf_op jit(solution)/shard_map/ppermute | solution.py:21
  42.2 3.4 %collective-permute-start.13 = (bf16[288,640]{1,0:T(8,128)(2,1)S(1)}, bf16[288,640]{1,0:T(8,128)(2,1)S(1)}, u32[]{:S(2)}, u32[]{:S(2)}) collective-permute-start(bf16[288,640]{1,0:T(8,128)(2,1)S(1)} %collective-permute-done.12.refs_2_), channel_id=1, source_target_pairs={{0,120},{8,0},{16,8},{24,16},{32,24},{40,32},{48,40},{56,48},{64,5... | collective-permute-start | bytes 1105928 | tf_op jit(solution)/shard_map/ppermute | solution.py:21
  45.6 5.6 %collective-permute-done.13.refs_2_ = bf16[288,640]{1,0:T(8,128)(2,1)S(1)} collective-permute-done((bf16[288,640]{1,0:T(8,128)(2,1)S(1)}, bf16[288,640]{1,0:T(8,128)(2,1)S(1)}, u32[]{:S(2)}, u32[]{:S(2)}) %collective-permute-start.13) | collective-permute-done | bytes 368672 | tf_op jit(solution)/shard_map/ppermute | solution.py:21
  51.2 3.4 %collective-permute-start.14 = (bf16[288,640]{1,0:T(8,128)(2,1)S(1)}, bf16[288,640]{1,0:T(8,128)(2,1)S(1)}, u32[]{:S(2)}, u32[]{:S(2)}) collective-permute-start(bf16[288,640]{1,0:T(8,128)(2,1)S(1)} %collective-permute-done.13.refs_2_), channel_id=1, source_target_pairs={{0,120},{8,0},{16,8},{24,16},{32,24},{40,32},{48,40},{56,48},{64,5... | collective-permute-start | bytes 1105928 | tf_op jit(solution)/shard_map/ppermute | solution.py:21
  54.6 4.8 %collective-permute-done.14.refs_2_ = bf16[288,640]{1,0:T(8,128)(2,1)S(1)} collective-permute-done((bf16[288,640]{1,0:T(8,128)(2,1)S(1)}, bf16[288,640]{1,0:T(8,128)(2,1)S(1)}, u32[]{:S(2)}, u32[]{:S(2)}) %collective-permute-start.14) | collective-permute-done | bytes 368672 | tf_op jit(solution)/shard_map/ppermute | solution.py:21
  59.4 3.4 %collective-permute-start.15 = (bf16[288,640]{1,0:T(8,128)(2,1)S(1)}, bf16[288,640]{1,0:T(8,128)(2,1)S(1)}, u32[]{:S(2)}, u32[]{:S(2)}) collective-permute-start(bf16[288,640]{1,0:T(8,128)(2,1)S(1)} %collective-permute-done.14.refs_2_), channel_id=1, source_target_pairs={{0,120},{8,0},{16,8},{24,16},{32,24},{40,32},{48,40},{56,48},{64,5... | collective-permute-start | bytes 1105928 | tf_op jit(solution)/shard_map/ppermute | solution.py:21
  62.8 4.5 %collective-permute-done.15.refs_2_ = bf16[288,640]{1,0:T(8,128)(2,1)S(1)} collective-permute-done((bf16[288,640]{1,0:T(8,128)(2,1)S(1)}, bf16[288,640]{1,0:T(8,128)(2,1)S(1)}, u32[]{:S(2)}, u32[]{:S(2)}) %collective-permute-start.15) | collective-permute-done | bytes 368672 | tf_op jit(solution)/shard_map/ppermute | solution.py:21
  67.2 3.1 %collective-permute-start.16 = (bf16[288,640]{1,0:T(8,128)(2,1)S(1)}, bf16[288,640]{1,0:T(8,128)(2,1)S(1)}, u32[]{:S(2)}, u32[]{:S(2)}) collective-permute-start(bf16[288,640]{1,0:T(8,128)(2,1)S(1)} %collective-permute-done.15.refs_2_), channel_id=1, source_target_pairs={{0,120},{8,0},{16,8},{24,16},{32,24},{40,32},{48,40},{56,48},{64,5... | collective-permute-start | bytes 1105928 | tf_op jit(solution)/shard_map/ppermute | solution.py:21
  70.4 1.3 collective-permute-start
  71.7 2.7 %collective-permute-start.1 = (bf16[144,640]{1,0:T(8,128)(2,1)}, bf16[144,640]{1,0:T(8,128)(2,1)S(1)}, u32[]{:S(2)}, u32[]{:S(2)}) collective-permute-start(bf16[144,640]{1,0:T(8,128)(2,1)} %param.4), channel_id=1, source_target_pairs={{0,4},{2,6},{4,0},{6,2},{1,5},{3,7},{5,1},{7,3},{8,12},{10,14},{12... | collective-permute-start | bytes 552968 | tf_op jit(solution)/shard_map/ppermute | solution.py:21
  74.4 1.0 collective-permute-start.2
  75.5 1.0 constant_dynamic-update-slice_fusion.3
  76.6 2.8 %collective-permute-start.17 = (bf16[288,640]{1,0:T(8,128)(2,1)S(1)}, bf16[288,640]{1,0:T(8,128)(2,1)S(1)}, u32[]{:S(2)}, u32[]{:S(2)}) collective-permute-start(bf16[288,640]{1,0:T(8,128)(2,1)S(1)} %collective-permute-done.16.refs_2_), channel_id=1, source_target_pairs={{0,120},{8,0},{16,8},{24,16},{32,24},{40,32},{48,40},{56,48},{64,5... | collective-permute-start | bytes 1105928 | tf_op jit(solution)/shard_map/ppermute | solution.py:21
  79.6 4.9 %attend.8 = (f32[16,640]{1,0:T(8,128)S(1)}, f32[16,640]{1,0:T(8,128)S(1)}, f32[704,640]{1,0:T(8,128)S(1)}) custom-call(bf16[640,640]{1,0:T(8,128)(2,1)S(1)} %broadcast_dynamic-update-slice_fusion.refs_0_, bf16[288,640]{1,0:T(8,128)(2,1)S(1)} %constant_dynamic-update-slice_fusion.4.refs_1_, bf16[288,640]{1,0:T(8,128)(2,1)S(1)} %collective-permute-done.3.refs_2_, ...), custom_call_target="tpu_custom_call" | custom-call | flops 707788800 | bytes 1638400 | tf_op jit(solution)/shard_map/attend/pallas_call | solution.py:160
  84.6 4.1 %attend.9 = (f32[16,640]{1,0:T(8,128)S(1)}, f32[16,640]{1,0:T(8,128)S(1)}, f32[704,640]{1,0:T(8,128)S(1)}) custom-call(bf16[640,640]{1,0:T(8,128)(2,1)S(1)} %broadcast_dynamic-update-slice_fusion.refs_0_, bf16[288,640]{1,0:T(8,128)(2,1)S(1)} %collective-permute-done.4.refs_1_, ...), custom_call_target="tpu_custom_call", output_to_operand_aliasing={{0}: (3, {}), {1}: (4, {}), {2}: (5, {})} | custom-call | flops 471859200 | bytes 1638400 | tf_op jit(solution)/shard_map/attend/pallas_call | solution.py:160
  89.2 2.8 %collective-permute-start.18 = (bf16[144,640]{1,0:T(8,128)(2,1)S(1)}, bf16[144,640]{1,0:T(8,128)(2,1)S(1)}, u32[]{:S(2)}, u32[]{:S(2)}) collective-permute-start(bf16[144,640]{1,0:T(8,128)(2,1)S(1)} %slice.9), channel_id=1, source_target_pairs={{0,120},{8,0},{16,8},{24,16},{32,24},{40,32},{48,40},{56,48},{64,5... | collective-permute-start | bytes 552968 | tf_op jit(solution)/shard_map/ppermute | solution.py:21
  91.9 4.1 %attend.10 = (f32[16,640]{1,0:T(8,128)S(1)}, f32[16,640]{1,0:T(8,128)S(1)}, f32[704,640]{1,0:T(8,128)S(1)}) custom-call(bf16[640,640]{1,0:T(8,128)(2,1)S(1)} %broadcast_dynamic-update-slice_fusion.refs_0_, bf16[288,640]{1,0:T(8,128)(2,1)S(1)} %collective-permute-done.5.refs_1_, ...), custom_call_target="tpu_custom_call", output_to_operand_aliasing={{0}: (3, {}), {1}: (4, {}), {2}: (5, {})} | custom-call | flops 471859200 | bytes 1638400 | tf_op jit(solution)/shard_map/attend/pallas_call | solution.py:160
  96.0 4.1 %attend.11 = (f32[16,640]{1,0:T(8,128)S(1)}, f32[16,640]{1,0:T(8,128)S(1)}, f32[704,640]{1,0:T(8,128)S(1)}) custom-call(bf16[640,640]{1,0:T(8,128)(2,1)S(1)} %broadcast_dynamic-update-slice_fusion.refs_0_, bf16[288,640]{1,0:T(8,128)(2,1)S(1)} %collective-permute-done.6.refs_1_, ...), custom_call_target="tpu_custom_call", output_to_operand_aliasing={{0}: (3, {}), {1}: (4, {}), {2}: (5, {})} | custom-call | flops 471859200 | bytes 1638400 | tf_op jit(solution)/shard_map/attend/pallas_call | solution.py:160
  100.0 4.1 %attend.12 = (f32[16,640]{1,0:T(8,128)S(1)}, f32[16,640]{1,0:T(8,128)S(1)}, f32[704,640]{1,0:T(8,128)S(1)}) custom-call(bf16[640,640]{1,0:T(8,128)(2,1)S(1)} %broadcast_dynamic-update-slice_fusion.refs_0_, bf16[288,640]{1,0:T(8,128)(2,1)S(1)} %collective-permute-done.7.refs_1_, ...), custom_call_target="tpu_custom_call", output_to_operand_aliasing={{0}: (3, {}), {1}: (4, {}), {2}: (5, {})} | custom-call | flops 471859200 | bytes 1638400 | tf_op jit(solution)/shard_map/attend/pallas_call | solution.py:160
  104.1 4.1 %attend.13 = (f32[16,640]{1,0:T(8,128)S(1)}, f32[16,640]{1,0:T(8,128)S(1)}, f32[704,640]{1,0:T(8,128)S(1)}) custom-call(bf16[640,640]{1,0:T(8,128)(2,1)S(1)} %broadcast_dynamic-update-slice_fusion.refs_0_, bf16[288,640]{1,0:T(8,128)(2,1)S(1)} %collective-permute-done.8.refs_1_, ...), custom_call_target="tpu_custom_call", output_to_operand_aliasing={{0}: (3, {}), {1}: (4, {}), {2}: (5, {})} | custom-call | flops 471859200 | bytes 1638400 | tf_op jit(solution)/shard_map/attend/pallas_call | solution.py:160
  108.2 4.1 %attend.14 = (f32[16,640]{1,0:T(8,128)S(1)}, f32[16,640]{1,0:T(8,128)S(1)}, f32[704,640]{1,0:T(8,128)S(1)}) custom-call(bf16[640,640]{1,0:T(8,128)(2,1)S(1)} %broadcast_dynamic-update-slice_fusion.refs_0_, bf16[288,640]{1,0:T(8,128)(2,1)S(1)} %collective-permute-done.9.refs_1_, ...), custom_call_target="tpu_custom_call", output_to_operand_aliasing={{0}: (3, {}), {1}: (4, {}), {2}: (5, {})} | custom-call | flops 471859200 | bytes 1638400 | tf_op jit(solution)/shard_map/attend/pallas_call | solution.py:160
  112.3 3.1 %attend.15 = (f32[16,640]{1,0:T(8,128)}, f32[16,640]{1,0:T(8,128)}, bf16[144,768]{1,0:T(8,128)(2,1)S(1)}, bf16[144,768]{1,0:T(8,128)(2,1)S(1)}, bf16[144,768]{1,...) custom-call(bf16[640,640]{1,0:T(8,128)(2,1)S(1)} %broadcast_dynamic-update-slice_fusion.refs_0_, ...), custom_call_target="tpu_custom_call" | custom-call | flops 235929600 | bytes 1638400 | tf_op jit(solution)/shard_map/attend/pallas_call | solution.py:160
  115.4 2.9 %collective-permute-start.19 = (bf16[144,768]{1,0:T(8,128)(2,1)S(1)}, bf16[144,768]{1,0:T(8,128)(2,1)S(1)}, u32[]{:S(2)}, u32[]{:S(2)}) collective-permute-start(bf16[144,768]{1,0:T(8,128)(2,1)S(1)} %get-tuple-element.52), channel_id=1, source_target_pairs={{0,6},{2,0},{4,2},{6,4},{1,7},{3,1},{5,3},{7,5},{8,14},{10,8},{12,... | collective-permute-start | bytes 663560 | tf_op jit(solution)/shard_map/ppermute | solution.py:21
  119.3 4.3 %collective-permute-done.19.refs_1_ = bf16[144,768]{1,0:T(8,128)(2,1)S(1)} collective-permute-done((bf16[144,768]{1,0:T(8,128)(2,1)S(1)}, bf16[144,768]{1,0:T(8,128)(2,1)S(1)}, u32[]{:S(2)}, u32[]{:S(2)}) %collective-permute-start.19) | collective-permute-done | bytes 221216 | tf_op jit(solution)/shard_map/ppermute | solution.py:21
  123.5 1.1 collective-permute-done.20.refs_2_
  124.7 2.2 %collective-permute-done.21.refs_3_ = bf16[144,768]{1,0:T(8,128)(2,1)S(1)} collective-permute-done((bf16[144,768]{1,0:T(8,128)(2,1)S(1)}, bf16[144,768]{1,0:T(8,128)(2,1)S(1)}, u32[]{:S(2)}, u32[]{:S(2)}) %collective-permute-start.21) | collective-permute-done | bytes 221216 | tf_op jit(solution)/shard_map/ppermute | solution.py:21
  126.9 1.6 %merge_project.1 = bf16[144,1280]{1,0:T(8,128)(2,1)S(1)} custom-call(bf16[144,768]{1,0:T(8,128)(2,1)S(1)} %get-tuple-element.51.refs_0_, bf16[144,768]{1,0:T(8,128)(2,1)S(1)} %collective-permute-done.19.refs_1_, bf16[144,768]{1,0:T(8,128)(2,1)S(1)} %collective-permute-done.20.refs_2_, bf16[144,768]{1,0:T(8,128)(2,1)S(1)} %collective-permute-done.21.refs_3_, ...), custom_call_target="tpu_custom_call" | custom-call | flops 235929600 | bytes 1638400 | tf_op jit(solution)/shard_map/merge_project/pallas_call | solution.py:219
  128.5 11.9 %collective-permute-start.22 = (bf16[72,1280]{1,0:T(8,128)(2,1)S(1)}, bf16[72,1280]{1,0:T(8,128)(2,1)S(1)}, u32[]{:S(2)}, u32[]{:S(2)}) collective-permute-start(bf16[72,1280]{1,0:T(8,128)(2,1)S(1)} %dynamic-slice_bitcast_fusion), channel_id=1, source_target_pairs={{0,1},{1,0},{2,3},{3,2},{4,5},{5,4},{6,7},{7,6},{8,9},{9,8},{10,11... | collective-permute-start | bytes 552968 | tf_op jit(solution)/shard_map/ppermute | solution.py:21
  140.4 1.1 collective-permute-done.22
  (36 shorter events, 4.5 us)
Async XLA Ops:
  1.9 30.4 %collective-permute-start.11 = (bf16[288,640]{1,0:T(8,128)(2,1)S(1)}, bf16[288,640]{1,0:T(8,128)(2,1)S(1)}, u32[]{:S(2)}, u32[]{:S(2)}) collective-permute-start(bf16[288,640]{1,0:T(8,128)(2,1)S(1)} %constant_dynamic-update-slice_fusion.4.refs_1_), channel_id=1, source_target_pairs={{0,120},{8,0},{16,8},{24,16},{32,24},{40,32},{48,40},{56,48},{64,5... | collective-permute-start | bytes 1105928 | tf_op jit(solution)/shard_map/ppermute | solution.py:21
  24.9 10.8 %collective-permute-start.3 = (bf16[288,640]{1,0:T(8,128)(2,1)S(1)}, bf16[288,640]{1,0:T(8,128)(2,1)S(1)}, u32[]{:S(2)}, u32[]{:S(2)}) collective-permute-start(bf16[288,640]{1,0:T(8,128)(2,1)S(1)} %constant_dynamic-update-slice_fusion.4.refs_1_), channel_id=1, source_target_pairs={{0,8},{8,16},{16,24},{24,32},{32,40},{40,48},{48,56},{56,64},{64,7... | collective-permute-start | bytes 1105928 | tf_op jit(solution)/shard_map/ppermute | solution.py:21
  32.3 9.9 %collective-permute-start.12 = (bf16[288,640]{1,0:T(8,128)(2,1)S(1)}, bf16[288,640]{1,0:T(8,128)(2,1)S(1)}, u32[]{:S(2)}, u32[]{:S(2)}) collective-permute-start(bf16[288,640]{1,0:T(8,128)(2,1)S(1)} %collective-permute-done.11.refs_3_), channel_id=1, source_target_pairs={{0,120},{8,0},{16,8},{24,16},{32,24},{40,32},{48,40},{56,48},{64,5... | collective-permute-start | bytes 1105928 | tf_op jit(solution)/shard_map/ppermute | solution.py:21
  35.7 9.9 %collective-permute-start.4 = (bf16[288,640]{1,0:T(8,128)(2,1)S(1)}, bf16[288,640]{1,0:T(8,128)(2,1)S(1)}, u32[]{:S(2)}, u32[]{:S(2)}) collective-permute-start(bf16[288,640]{1,0:T(8,128)(2,1)S(1)} %collective-permute-done.3.refs_2_), channel_id=1, source_target_pairs={{0,8},{8,16},{16,24},{24,32},{32,40},{40,48},{48,56},{56,64},{64,7... | collective-permute-start | bytes 1105928 | tf_op jit(solution)/shard_map/ppermute | solution.py:21
  42.2 9.0 %collective-permute-start.13 = (bf16[288,640]{1,0:T(8,128)(2,1)S(1)}, bf16[288,640]{1,0:T(8,128)(2,1)S(1)}, u32[]{:S(2)}, u32[]{:S(2)}) collective-permute-start(bf16[288,640]{1,0:T(8,128)(2,1)S(1)} %collective-permute-done.12.refs_2_), channel_id=1, source_target_pairs={{0,120},{8,0},{16,8},{24,16},{32,24},{40,32},{48,40},{56,48},{64,5... | collective-permute-start | bytes 1105928 | tf_op jit(solution)/shard_map/ppermute | solution.py:21
  45.6 9.0 %collective-permute-start.5 = (bf16[288,640]{1,0:T(8,128)(2,1)S(1)}, bf16[288,640]{1,0:T(8,128)(2,1)S(1)}, u32[]{:S(2)}, u32[]{:S(2)}) collective-permute-start(bf16[288,640]{1,0:T(8,128)(2,1)S(1)} %collective-permute-done.4.refs_1_), channel_id=1, source_target_pairs={{0,8},{8,16},{16,24},{24,32},{32,40},{40,48},{48,56},{56,64},{64,7... | collective-permute-start | bytes 1105928 | tf_op jit(solution)/shard_map/ppermute | solution.py:21
  51.2 8.2 %collective-permute-start.14 = (bf16[288,640]{1,0:T(8,128)(2,1)S(1)}, bf16[288,640]{1,0:T(8,128)(2,1)S(1)}, u32[]{:S(2)}, u32[]{:S(2)}) collective-permute-start(bf16[288,640]{1,0:T(8,128)(2,1)S(1)} %collective-permute-done.13.refs_2_), channel_id=1, source_target_pairs={{0,120},{8,0},{16,8},{24,16},{32,24},{40,32},{48,40},{56,48},{64,5... | collective-permute-start | bytes 1105928 | tf_op jit(solution)/shard_map/ppermute | solution.py:21
  54.6 8.2 %collective-permute-start.6 = (bf16[288,640]{1,0:T(8,128)(2,1)S(1)}, bf16[288,640]{1,0:T(8,128)(2,1)S(1)}, u32[]{:S(2)}, u32[]{:S(2)}) collective-permute-start(bf16[288,640]{1,0:T(8,128)(2,1)S(1)} %collective-permute-done.5.refs_1_), channel_id=1, source_target_pairs={{0,8},{8,16},{16,24},{24,32},{32,40},{40,48},{48,56},{56,64},{64,7... | collective-permute-start | bytes 1105928 | tf_op jit(solution)/shard_map/ppermute | solution.py:21
  59.4 7.9 %collective-permute-start.15 = (bf16[288,640]{1,0:T(8,128)(2,1)S(1)}, bf16[288,640]{1,0:T(8,128)(2,1)S(1)}, u32[]{:S(2)}, u32[]{:S(2)}) collective-permute-start(bf16[288,640]{1,0:T(8,128)(2,1)S(1)} %collective-permute-done.14.refs_2_), channel_id=1, source_target_pairs={{0,120},{8,0},{16,8},{24,16},{32,24},{40,32},{48,40},{56,48},{64,5... | collective-permute-start | bytes 1105928 | tf_op jit(solution)/shard_map/ppermute | solution.py:21
  62.8 7.6 %collective-permute-start.7 = (bf16[288,640]{1,0:T(8,128)(2,1)S(1)}, bf16[288,640]{1,0:T(8,128)(2,1)S(1)}, u32[]{:S(2)}, u32[]{:S(2)}) collective-permute-start(bf16[288,640]{1,0:T(8,128)(2,1)S(1)} %collective-permute-done.6.refs_1_), channel_id=1, source_target_pairs={{0,8},{8,16},{16,24},{24,32},{32,40},{40,48},{48,56},{56,64},{64,7... | collective-permute-start | bytes 1105928 | tf_op jit(solution)/shard_map/ppermute | solution.py:21
  67.2 9.4 %collective-permute-start.16 = (bf16[288,640]{1,0:T(8,128)(2,1)S(1)}, bf16[288,640]{1,0:T(8,128)(2,1)S(1)}, u32[]{:S(2)}, u32[]{:S(2)}) collective-permute-start(bf16[288,640]{1,0:T(8,128)(2,1)S(1)} %collective-permute-done.15.refs_2_), channel_id=1, source_target_pairs={{0,120},{8,0},{16,8},{24,16},{32,24},{40,32},{48,40},{56,48},{64,5... | collective-permute-start | bytes 1105928 | tf_op jit(solution)/shard_map/ppermute | solution.py:21
  70.4 9.1 %collective-permute-start.8 = (bf16[288,640]{1,0:T(8,128)(2,1)S(1)}, bf16[288,640]{1,0:T(8,128)(2,1)S(1)}, u32[]{:S(2)}, u32[]{:S(2)}) collective-permute-start(bf16[288,640]{1,0:T(8,128)(2,1)S(1)} %collective-permute-done.7.refs_1_), channel_id=1, source_target_pairs={{0,8},{8,16},{16,24},{24,32},{32,40},{40,48},{48,56},{56,64},{64,7... | collective-permute-start | bytes 1105928 | tf_op jit(solution)/shard_map/ppermute | solution.py:21
  70.4 6.2 %collective-permute-start = (bf16[144,640]{1,0:T(8,128)(2,1)}, bf16[144,640]{1,0:T(8,128)(2,1)S(1)}, u32[]{:S(2)}, u32[]{:S(2)}) collective-permute-start(bf16[144,640]{1,0:T(8,128)(2,1)} %param.4), channel_id=1, source_target_pairs={{0,2},{2,4},{4,6},{6,0},{1,3},{3,5},{5,7},{7,1},{8,10},{10,12},{12... | collective-permute-start | bytes 552968 | tf_op jit(solution)/shard_map/ppermute | solution.py:21
  71.7 7.8 %collective-permute-start.1 = (bf16[144,640]{1,0:T(8,128)(2,1)}, bf16[144,640]{1,0:T(8,128)(2,1)S(1)}, u32[]{:S(2)}, u32[]{:S(2)}) collective-permute-start(bf16[144,640]{1,0:T(8,128)(2,1)} %param.4), channel_id=1, source_target_pairs={{0,4},{2,6},{4,0},{6,2},{1,5},{3,7},{5,1},{7,3},{8,12},{10,14},{12... | collective-permute-start | bytes 552968 | tf_op jit(solution)/shard_map/ppermute | solution.py:21
  74.4 5.1 %collective-permute-start.2 = (bf16[144,640]{1,0:T(8,128)(2,1)}, bf16[144,640]{1,0:T(8,128)(2,1)S(1)}, u32[]{:S(2)}, u32[]{:S(2)}) collective-permute-start(bf16[144,640]{1,0:T(8,128)(2,1)} %param.4), channel_id=1, source_target_pairs={{0,6},{2,0},{4,2},{6,4},{1,7},{3,1},{5,3},{7,5},{8,14},{10,8},{12,... | collective-permute-start | bytes 552968 | tf_op jit(solution)/shard_map/ppermute | solution.py:21
  76.6 12.5 %collective-permute-start.17 = (bf16[288,640]{1,0:T(8,128)(2,1)S(1)}, bf16[288,640]{1,0:T(8,128)(2,1)S(1)}, u32[]{:S(2)}, u32[]{:S(2)}) collective-permute-start(bf16[288,640]{1,0:T(8,128)(2,1)S(1)} %collective-permute-done.16.refs_2_), channel_id=1, source_target_pairs={{0,120},{8,0},{16,8},{24,16},{32,24},{40,32},{48,40},{56,48},{64,5... | collective-permute-start | bytes 1105928 | tf_op jit(solution)/shard_map/ppermute | solution.py:21
  79.5 9.5 %collective-permute-start.9 = (bf16[288,640]{1,0:T(8,128)(2,1)S(1)}, bf16[288,640]{1,0:T(8,128)(2,1)S(1)}, u32[]{:S(2)}, u32[]{:S(2)}) collective-permute-start(bf16[288,640]{1,0:T(8,128)(2,1)S(1)} %collective-permute-done.8.refs_1_), channel_id=1, source_target_pairs={{0,8},{8,16},{16,24},{24,32},{32,40},{40,48},{48,56},{56,64},{64,7... | collective-permute-start | bytes 1105928 | tf_op jit(solution)/shard_map/ppermute | solution.py:21
  89.0 23.3 %collective-permute-start.10 = (bf16[144,640]{1,0:T(8,128)(2,1)S(1)}, bf16[144,640]{1,0:T(8,128)(2,1)S(1)}, u32[]{:S(2)}, u32[]{:S(2)}) collective-permute-start(bf16[144,640]{1,0:T(8,128)(2,1)S(1)} %slice.8), channel_id=1, source_target_pairs={{0,8},{8,16},{16,24},{24,32},{32,40},{40,48},{48,56},{56,64},{64,7... | collective-permute-start | bytes 552968 | tf_op jit(solution)/shard_map/ppermute | solution.py:21
  89.2 23.1 %collective-permute-start.18 = (bf16[144,640]{1,0:T(8,128)(2,1)S(1)}, bf16[144,640]{1,0:T(8,128)(2,1)S(1)}, u32[]{:S(2)}, u32[]{:S(2)}) collective-permute-start(bf16[144,640]{1,0:T(8,128)(2,1)S(1)} %slice.9), channel_id=1, source_target_pairs={{0,120},{8,0},{16,8},{24,16},{32,24},{40,32},{48,40},{56,48},{64,5... | collective-permute-start | bytes 552968 | tf_op jit(solution)/shard_map/ppermute | solution.py:21
  112.3 14.6 %copy-start = (bf16[640,1280]{1,0:T(8,128)(2,1)S(1)}, bf16[640,1280]{1,0:T(8,128)(2,1)}, u32[]{:S(2)}) copy-start(bf16[640,1280]{1,0:T(8,128)(2,1)} %refs_4_.1) | copy-start | bytes 4915204
  115.4 8.1 %collective-permute-start.19 = (bf16[144,768]{1,0:T(8,128)(2,1)S(1)}, bf16[144,768]{1,0:T(8,128)(2,1)S(1)}, u32[]{:S(2)}, u32[]{:S(2)}) collective-permute-start(bf16[144,768]{1,0:T(8,128)(2,1)S(1)} %get-tuple-element.52), channel_id=1, source_target_pairs={{0,6},{2,0},{4,2},{6,4},{1,7},{3,1},{5,3},{7,5},{8,14},{10,8},{12,... | collective-permute-start | bytes 663560 | tf_op jit(solution)/shard_map/ppermute | solution.py:21
  118.3 6.4 %collective-permute-start.20 = (bf16[144,768]{1,0:T(8,128)(2,1)S(1)}, bf16[144,768]{1,0:T(8,128)(2,1)S(1)}, u32[]{:S(2)}, u32[]{:S(2)}) collective-permute-start(bf16[144,768]{1,0:T(8,128)(2,1)S(1)} %get-tuple-element.53), channel_id=1, source_target_pairs={{0,4},{2,6},{4,0},{6,2},{1,5},{3,7},{5,1},{7,3},{8,12},{10,14},{12... | collective-permute-start | bytes 663560 | tf_op jit(solution)/shard_map/ppermute | solution.py:21
  118.5 8.4 %collective-permute-start.21 = (bf16[144,768]{1,0:T(8,128)(2,1)S(1)}, bf16[144,768]{1,0:T(8,128)(2,1)S(1)}, u32[]{:S(2)}, u32[]{:S(2)}) collective-permute-start(bf16[144,768]{1,0:T(8,128)(2,1)S(1)} %get-tuple-element.54), channel_id=1, source_target_pairs={{0,2},{2,4},{4,6},{6,0},{1,3},{3,5},{5,7},{7,1},{8,10},{10,12},{12... | collective-permute-start | bytes 663560 | tf_op jit(solution)/shard_map/ppermute | solution.py:21
  128.5 12.9 %collective-permute-start.22 = (bf16[72,1280]{1,0:T(8,128)(2,1)S(1)}, bf16[72,1280]{1,0:T(8,128)(2,1)S(1)}, u32[]{:S(2)}, u32[]{:S(2)}) collective-permute-start(bf16[72,1280]{1,0:T(8,128)(2,1)S(1)} %dynamic-slice_bitcast_fusion), channel_id=1, source_target_pairs={{0,1},{1,0},{2,3},{3,2},{4,5},{5,4},{6,7},{7,6},{8,9},{9,8},{10,11... | collective-permute-start | bytes 552968 | tf_op jit(solution)/shard_map/ppermute | solution.py:21
where the time goes:
time: 142 us
  starting transfers between devices  66.4 us (47%)
  waiting for transfers between devices  37.9 us (27%)
  Pallas kernels  34 us (24%)
  local copies, waits for them, and re-layouts  3 us (2%)
    ppermute x23, starting transfers between devices, shifted(): lax.ppermute(array, axis, [(i, (i + by) % size) for i in range(size)])  66.4 us
    ppermute x23, waiting for transfers between devices, shifted(): lax.ppermute(array, axis, [(i, (i + by) % size) for i in range(size)])  37.9 us
    pallas_call x8, Pallas kernels, attend_step(): pl.pallas_call(body, out_shape=outs, in_specs=[vmem] * inputs, out_specs=...  32.5 us
  transfers between devices with their start and end apart: 23, of which 12 were waited for; matrix products, arithmetic and copies ran while one was open for 1% of the time, Pallas kernels for 21%

commit v1 on v0

--- a/solution.py
+++ b/solution.py
@@ -240,22 +240,32 @@
     def piece(both):
         return (both, 0, both, rows, rows)
 
-    own = jnp.concatenate([key, value], axis=0)
-    up = down = own
-    held = [piece(own)]
+    up = down = None
+    held = [(key, 0, value, 0, rows)]
     state = None
     for turn in range(1, half + 1):
         final = turn == half
+        if turn > 1:
+            up, down = lax.optimization_barrier((up, down))
+            held = held[: len(held) - 2] + [piece(up), piece(down)]
         if final:
             k = shifted(up[:rows], "blk", 1)
             v = shifted(down[rows:], "blk", -1)
             arrived = [(k, 0, v, 0, rows)]
+        elif turn == 1:
+            k_up, k_down = shifted(key, "blk", 1), shifted(key, "blk", -1)
+            v_up, v_down = shifted(value, "blk", 1), shifted(value, "blk", -1)
+            up = jnp.concatenate([k_up, v_up], axis=0)
+            down = jnp.concatenate([k_down, v_down], axis=0)
         else:
             up = shifted(up, "blk", 1)
             down = shifted(down, "blk", -1)
+        if not final:
             arrived = [piece(up), piece(down)]
         if turn == 1:
-            stack = [query] + [shifted(query, "node", d) for d in range(1, nodes)]
+            turns = sorted(range(1, nodes), key=lambda d: -min(d, nodes - d))
+            others = {d: shifted(query, "node", d) for d in turns}
+            stack = [query] + [others[d] for d in range(1, nodes)]
             blocks = [rows] * nodes
             padded = round_up(rows * nodes, LANES)
             if padded > rows * nodes:
@@ -267,7 +277,7 @@
         held = held + arrived
 
     parts = list(attend_step(queries, held, state, True, blocks)[2:])
-    for d in range(1, nodes):
+    for d in turns:
         parts[d] = shifted(parts[d], "node", -d)
     mine = merge_project(parts, out_weight)
 

time: 142 us -> 143 us (level)
  waiting for transfers between devices: 37.9 us -> 42.3 us
  starting transfers between devices: 66.4 us -> 64.3 us
  local copies, waits for them, and re-layouts: 3 us -> 1.13 us
    ppermute x23 -> x25, waiting for transfers between devices: 37.9 us -> 42.3 us  [shifted(): lax.ppermute(array, axis, [(i, (i + by) % size) for i in range(size)])]
    ppermute x23 -> x25, starting transfers between devices: 66.4 us -> 64.3 us  [shifted(): lax.ppermute(array, axis, [(i, (i + by) % size) for i in range(size)])]
  transfers between devices with their start and end apart: 23 -> 25, of which waited for: 12 -> 12; matrix products, arithmetic and copies ran while one was open for 1% -> 1% of each run, Pallas kernels for 21% -> 21%
where the time goes in v1:
time: 143 us
  starting transfers between devices  64.3 us (45%)
  waiting for transfers between devices  42.3 us (30%)
  Pallas kernels  34 us (24%)
    ppermute x25, starting transfers between devices, shifted(): lax.ppermute(array, axis, [(i, (i + by) % size) for i in range(size)])  64.3 us
    ppermute x25, waiting for transfers between devices, shifted(): lax.ppermute(array, axis, [(i, (i + by) % size) for i in range(size)])  42.3 us
    pallas_call x8, Pallas kernels, attend_step(): pl.pallas_call(body, out_shape=outs, in_specs=[vmem] * inputs, out_specs=...  32.4 us
  transfers between devices with their start and end apart: 25, of which 12 were waited for; matrix products, arithmetic and copies ran while one was open for 1% of the time, Pallas kernels for 21%

profile of v1, /device:TPU:33, one launch (start us, length us, event | category | flops | bytes accessed | tf_op | source)
XLA Modules:
  0.0 142.8 jit_solution(857673892808416546)
XLA Ops:
  0.0 3.3 %collective-permute-start.3 = (bf16[144,640]{1,0:T(8,128)(2,1)}, bf16[144,640]{1,0:T(8,128)(2,1)S(1)}, u32[]{:S(2)}, u32[]{:S(2)}) collective-permute-start(bf16[144,640]{1,0:T(8,128)(2,1)} %refs_1_.1), channel_id=1, source_target_pairs={{0,8},{8,16},{16,24},{24,32},{32,40},{40,48},{48,56},{56,64},{64,7... | collective-permute-start | bytes 552968 | tf_op jit(solution)/shard_map/ppermute | solution.py:21
  3.3 2.5 %collective-permute-start.4 = (bf16[144,640]{1,0:T(8,128)(2,1)}, bf16[144,640]{1,0:T(8,128)(2,1)S(1)}, u32[]{:S(2)}, u32[]{:S(2)}) collective-permute-start(bf16[144,640]{1,0:T(8,128)(2,1)} %refs_2_.1), channel_id=1, source_target_pairs={{0,8},{8,16},{16,24},{24,32},{32,40},{40,48},{48,56},{56,64},{64,7... | collective-permute-start | bytes 552968 | tf_op jit(solution)/shard_map/ppermute | solution.py:21
  5.8 17.4 %collective-permute-start.5 = (bf16[144,640]{1,0:T(8,128)(2,1)}, bf16[144,640]{1,0:T(8,128)(2,1)S(1)}, u32[]{:S(2)}, u32[]{:S(2)}) collective-permute-start(bf16[144,640]{1,0:T(8,128)(2,1)} %refs_1_.1), channel_id=1, source_target_pairs={{0,120},{8,0},{16,8},{24,16},{32,24},{40,32},{48,40},{56,48},{64,5... | collective-permute-start | bytes 552968 | tf_op jit(solution)/shard_map/ppermute | solution.py:21
  24.5 3.1 %collective-permute-done.3 = bf16[144,640]{1,0:T(8,128)(2,1)S(1)} collective-permute-done((bf16[144,640]{1,0:T(8,128)(2,1)}, bf16[144,640]{1,0:T(8,128)(2,1)S(1)}, u32[]{:S(2)}, u32[]{:S(2)}) %collective-permute-start.3) | collective-permute-done | bytes 184352 | tf_op jit(solution)/shard_map/ppermute | solution.py:21
  27.6 3.9 %collective-permute-done.4 = bf16[144,640]{1,0:T(8,128)(2,1)S(1)} collective-permute-done((bf16[144,640]{1,0:T(8,128)(2,1)}, bf16[144,640]{1,0:T(8,128)(2,1)S(1)}, u32[]{:S(2)}, u32[]{:S(2)}) %collective-permute-start.4) | collective-permute-done | bytes 184352 | tf_op jit(solution)/shard_map/ppermute | solution.py:21
  31.8 2.6 %collective-permute-start.8 = (bf16[288,640]{1,0:T(8,128)(2,1)S(1)}, bf16[288,640]{1,0:T(8,128)(2,1)S(1)}, u32[]{:S(2)}, u32[]{:S(2)}) collective-permute-start(bf16[288,640]{1,0:T(8,128)(2,1)S(1)} %pad_maximum_fusion.1.refs_4_), channel_id=1, source_target_pairs={{0,120},{8,0},{16,8},{24,16},{32,24},{40,32},{48,40},{56,48},{64,5... | collective-permute-start | bytes 1105928 | tf_op jit(solution)/shard_map/ppermute | solution.py:21
  34.4 7.5 %collective-permute-done.7.refs_1_ = bf16[288,640]{1,0:T(8,128)(2,1)S(1)} collective-permute-done((bf16[288,640]{1,0:T(8,128)(2,1)S(1)}, bf16[288,640]{1,0:T(8,128)(2,1)S(1)}, u32[]{:S(2)}, u32[]{:S(2)}) %collective-permute-start.7) | collective-permute-done | bytes 368672 | tf_op jit(solution)/shard_map/ppermute | solution.py:21
  41.9 2.4 %collective-permute-start.10 = (bf16[288,640]{1,0:T(8,128)(2,1)S(1)}, bf16[288,640]{1,0:T(8,128)(2,1)S(1)}, u32[]{:S(2)}, u32[]{:S(2)}) collective-permute-start(bf16[288,640]{1,0:T(8,128)(2,1)S(1)} %collective-permute-done.8.refs_2_), channel_id=1, source_target_pairs={{0,120},{8,0},{16,8},{24,16},{32,24},{40,32},{48,40},{56,48},{64,5... | collective-permute-start | bytes 1105928 | tf_op jit(solution)/shard_map/ppermute | solution.py:21
  44.3 5.7 %collective-permute-done.10.refs_2_ = bf16[288,640]{1,0:T(8,128)(2,1)S(1)} collective-permute-done((bf16[288,640]{1,0:T(8,128)(2,1)S(1)}, bf16[288,640]{1,0:T(8,128)(2,1)S(1)}, u32[]{:S(2)}, u32[]{:S(2)}) %collective-permute-start.10) | collective-permute-done | bytes 368672 | tf_op jit(solution)/shard_map/ppermute | solution.py:21
  50.1 3.0 %collective-permute-done.9.refs_1_ = bf16[288,640]{1,0:T(8,128)(2,1)S(1)} collective-permute-done((bf16[288,640]{1,0:T(8,128)(2,1)S(1)}, bf16[288,640]{1,0:T(8,128)(2,1)S(1)}, u32[]{:S(2)}, u32[]{:S(2)}) %collective-permute-start.9) | collective-permute-done | bytes 368672 | tf_op jit(solution)/shard_map/ppermute | solution.py:21
  53.1 2.7 %collective-permute-start.12 = (bf16[288,640]{1,0:T(8,128)(2,1)S(1)}, bf16[288,640]{1,0:T(8,128)(2,1)S(1)}, u32[]{:S(2)}, u32[]{:S(2)}) collective-permute-start(bf16[288,640]{1,0:T(8,128)(2,1)S(1)} %collective-permute-done.10.refs_2_), channel_id=1, source_target_pairs={{0,120},{8,0},{16,8},{24,16},{32,24},{40,32},{48,40},{56,48},{64,5... | collective-permute-start | bytes 1105928 | tf_op jit(solution)/shard_map/ppermute | solution.py:21
  55.8 5.2 %collective-permute-done.11.refs_1_ = bf16[288,640]{1,0:T(8,128)(2,1)S(1)} collective-permute-done((bf16[288,640]{1,0:T(8,128)(2,1)S(1)}, bf16[288,640]{1,0:T(8,128)(2,1)S(1)}, u32[]{:S(2)}, u32[]{:S(2)}) %collective-permute-start.11) | collective-permute-done | bytes 368672 | tf_op jit(solution)/shard_map/ppermute | solution.py:21
  61.0 2.7 %collective-permute-start.14 = (bf16[288,640]{1,0:T(8,128)(2,1)S(1)}, bf16[288,640]{1,0:T(8,128)(2,1)S(1)}, u32[]{:S(2)}, u32[]{:S(2)}) collective-permute-start(bf16[288,640]{1,0:T(8,128)(2,1)S(1)} %collective-permute-done.12.refs_2_), channel_id=1, source_target_pairs={{0,120},{8,0},{16,8},{24,16},{32,24},{40,32},{48,40},{56,48},{64,5... | collective-permute-start | bytes 1105928 | tf_op jit(solution)/shard_map/ppermute | solution.py:21
  63.7 4.9 %collective-permute-done.13.refs_1_ = bf16[288,640]{1,0:T(8,128)(2,1)S(1)} collective-permute-done((bf16[288,640]{1,0:T(8,128)(2,1)S(1)}, bf16[288,640]{1,0:T(8,128)(2,1)S(1)}, u32[]{:S(2)}, u32[]{:S(2)}) %collective-permute-start.13) | collective-permute-done | bytes 368672 | tf_op jit(solution)/shard_map/ppermute | solution.py:21
  68.6 2.9 %collective-permute-start.16 = (bf16[288,640]{1,0:T(8,128)(2,1)S(1)}, bf16[288,640]{1,0:T(8,128)(2,1)S(1)}, u32[]{:S(2)}, u32[]{:S(2)}) collective-permute-start(bf16[288,640]{1,0:T(8,128)(2,1)S(1)} %collective-permute-done.14.refs_2_), channel_id=1, source_target_pairs={{0,120},{8,0},{16,8},{24,16},{32,24},{40,32},{48,40},{56,48},{64,5... | collective-permute-start | bytes 1105928 | tf_op jit(solution)/shard_map/ppermute | solution.py:21
  71.5 1.3 collective-permute-start
  72.8 2.7 %collective-permute-start.1 = (bf16[144,640]{1,0:T(8,128)(2,1)}, bf16[144,640]{1,0:T(8,128)(2,1)S(1)}, u32[]{:S(2)}, u32[]{:S(2)}) collective-permute-start(bf16[144,640]{1,0:T(8,128)(2,1)} %param.4), channel_id=1, source_target_pairs={{0,4},{2,6},{4,0},{6,2},{1,5},{3,7},{5,1},{7,3},{8,12},{10,14},{12... | collective-permute-start | bytes 552968 | tf_op jit(solution)/shard_map/ppermute | solution.py:21
  77.8 2.7 %collective-permute-start.18 = (bf16[288,640]{1,0:T(8,128)(2,1)S(1)}, bf16[288,640]{1,0:T(8,128)(2,1)S(1)}, u32[]{:S(2)}, u32[]{:S(2)}) collective-permute-start(bf16[288,640]{1,0:T(8,128)(2,1)S(1)} %collective-permute-done.16.refs_2_), channel_id=1, source_target_pairs={{0,120},{8,0},{16,8},{24,16},{32,24},{40,32},{48,40},{56,48},{64,5... | collective-permute-start | bytes 1105928 | tf_op jit(solution)/shard_map/ppermute | solution.py:21
  80.8 4.9 %attend.8 = (f32[16,640]{1,0:T(8,128)S(1)}, f32[16,640]{1,0:T(8,128)S(1)}, f32[704,640]{1,0:T(8,128)S(1)}) custom-call(bf16[640,640]{1,0:T(8,128)(2,1)S(1)} %broadcast_dynamic-update-slice_fusion.refs_0_, bf16[144,640]{1,0:T(8,128)(2,1)S(1)} %copy-done.2, bf16[144,640]{1,0:T(8,128)(2,1)S(1)} %copy-done.1, bf16[288,640]{1,0:T(8,128)(2,1)S(1)} %pad_maximum_fusion.refs_3_, ...), custom_call_target="tpu_custom_call" | custom-call | flops 707788800 | bytes 1638400 | tf_op jit(solution)/shard_map/attend/pallas_call | solution.py:160
  85.7 4.1 %attend.9 = (f32[16,640]{1,0:T(8,128)S(1)}, f32[16,640]{1,0:T(8,128)S(1)}, f32[704,640]{1,0:T(8,128)S(1)}) custom-call(bf16[640,640]{1,0:T(8,128)(2,1)S(1)} %broadcast_dynamic-update-slice_fusion.refs_0_, bf16[288,640]{1,0:T(8,128)(2,1)S(1)} %collective-permute-done.7.refs_1_, ...), custom_call_target="tpu_custom_call", output_to_operand_aliasing={{0}: (3, {}), {1}: (4, {}), {2}: (5, {})} | custom-call | flops 471859200 | bytes 1638400 | tf_op jit(solution)/shard_map/attend/pallas_call | solution.py:160
  90.0 2.8 %collective-permute-start.20 = (bf16[144,640]{1,0:T(8,128)(2,1)S(1)}, bf16[144,640]{1,0:T(8,128)(2,1)S(1)}, u32[]{:S(2)}, u32[]{:S(2)}) collective-permute-start(bf16[144,640]{1,0:T(8,128)(2,1)S(1)} %slice.7), channel_id=1, source_target_pairs={{0,120},{8,0},{16,8},{24,16},{32,24},{40,32},{48,40},{56,48},{64,5... | collective-permute-start | bytes 552968 | tf_op jit(solution)/shard_map/ppermute | solution.py:21
  92.8 4.1 %attend.10 = (f32[16,640]{1,0:T(8,128)S(1)}, f32[16,640]{1,0:T(8,128)S(1)}, f32[704,640]{1,0:T(8,128)S(1)}) custom-call(bf16[640,640]{1,0:T(8,128)(2,1)S(1)} %broadcast_dynamic-update-slice_fusion.refs_0_, bf16[288,640]{1,0:T(8,128)(2,1)S(1)} %collective-permute-done.9.refs_1_, ...), custom_call_target="tpu_custom_call", output_to_operand_aliasing={{0}: (3, {}), {1}: (4, {}), {2}: (5, {})} | custom-call | flops 471859200 | bytes 1638400 | tf_op jit(solution)/shard_map/attend/pallas_call | solution.py:160
  96.8 4.1 %attend.11 = (f32[16,640]{1,0:T(8,128)S(1)}, f32[16,640]{1,0:T(8,128)S(1)}, f32[704,640]{1,0:T(8,128)S(1)}) custom-call(bf16[640,640]{1,0:T(8,128)(2,1)S(1)} %broadcast_dynamic-update-slice_fusion.refs_0_, bf16[288,640]{1,0:T(8,128)(2,1)S(1)} %collective-permute-done.11.refs_1_, ...), custom_call_target="tpu_custom_call", output_to_operand_aliasing={{0}: (3, {}), {1}: (4, {}), {2}: (5, {})} | custom-call | flops 471859200 | bytes 1638400 | tf_op jit(solution)/shard_map/attend/pallas_call | solution.py:160
  100.9 4.1 %attend.12 = (f32[16,640]{1,0:T(8,128)S(1)}, f32[16,640]{1,0:T(8,128)S(1)}, f32[704,640]{1,0:T(8,128)S(1)}) custom-call(bf16[640,640]{1,0:T(8,128)(2,1)S(1)} %broadcast_dynamic-update-slice_fusion.refs_0_, bf16[288,640]{1,0:T(8,128)(2,1)S(1)} %collective-permute-done.13.refs_1_, ...), custom_call_target="tpu_custom_call", output_to_operand_aliasing={{0}: (3, {}), {1}: (4, {}), {2}: (5, {})} | custom-call | flops 471859200 | bytes 1638400 | tf_op jit(solution)/shard_map/attend/pallas_call | solution.py:160
  105.0 4.1 %attend.13 = (f32[16,640]{1,0:T(8,128)S(1)}, f32[16,640]{1,0:T(8,128)S(1)}, f32[704,640]{1,0:T(8,128)S(1)}) custom-call(bf16[640,640]{1,0:T(8,128)(2,1)S(1)} %broadcast_dynamic-update-slice_fusion.refs_0_, bf16[288,640]{1,0:T(8,128)(2,1)S(1)} %collective-permute-done.15.refs_1_, ...), custom_call_target="tpu_custom_call", output_to_operand_aliasing={{0}: (3, {}), {1}: (4, {}), {2}: (5, {})} | custom-call | flops 471859200 | bytes 1638400 | tf_op jit(solution)/shard_map/attend/pallas_call | solution.py:160
  109.0 4.1 %attend.14 = (f32[16,640]{1,0:T(8,128)S(1)}, f32[16,640]{1,0:T(8,128)S(1)}, f32[704,640]{1,0:T(8,128)S(1)}) custom-call(bf16[640,640]{1,0:T(8,128)(2,1)S(1)} %broadcast_dynamic-update-slice_fusion.refs_0_, bf16[288,640]{1,0:T(8,128)(2,1)S(1)} %collective-permute-done.17.refs_1_, ...), custom_call_target="tpu_custom_call", output_to_operand_aliasing={{0}: (3, {}), {1}: (4, {}), {2}: (5, {})} | custom-call | flops 471859200 | bytes 1638400 | tf_op jit(solution)/shard_map/attend/pallas_call | solution.py:160
  113.1 3.1 %attend.15 = (f32[16,640]{1,0:T(8,128)}, f32[16,640]{1,0:T(8,128)}, bf16[144,768]{1,0:T(8,128)(2,1)S(1)}, bf16[144,768]{1,0:T(8,128)(2,1)S(1)}, bf16[144,768]{1,...) custom-call(bf16[640,640]{1,0:T(8,128)(2,1)S(1)} %broadcast_dynamic-update-slice_fusion.refs_0_, ...), custom_call_target="tpu_custom_call" | custom-call | flops 235929600 | bytes 1638400 | tf_op jit(solution)/shard_map/attend/pallas_call | solution.py:160
  116.2 2.7 %collective-permute-start.21 = (bf16[144,768]{1,0:T(8,128)(2,1)S(1)}, bf16[144,768]{1,0:T(8,128)(2,1)S(1)}, u32[]{:S(2)}, u32[]{:S(2)}) collective-permute-start(bf16[144,768]{1,0:T(8,128)(2,1)S(1)} %get-tuple-element.80), channel_id=1, source_target_pairs={{0,6},{2,0},{4,2},{6,4},{1,7},{3,1},{5,3},{7,5},{8,14},{10,8},{12,... | collective-permute-start | bytes 663560 | tf_op jit(solution)/shard_map/ppermute | solution.py:21
  119.9 4.3 %collective-permute-done.21.refs_1_ = bf16[144,768]{1,0:T(8,128)(2,1)S(1)} collective-permute-done((bf16[144,768]{1,0:T(8,128)(2,1)S(1)}, bf16[144,768]{1,0:T(8,128)(2,1)S(1)}, u32[]{:S(2)}, u32[]{:S(2)}) %collective-permute-start.21) | collective-permute-done | bytes 221216 | tf_op jit(solution)/shard_map/ppermute | solution.py:21
  125.3 2.2 %collective-permute-done.23.refs_3_ = bf16[144,768]{1,0:T(8,128)(2,1)S(1)} collective-permute-done((bf16[144,768]{1,0:T(8,128)(2,1)S(1)}, bf16[144,768]{1,0:T(8,128)(2,1)S(1)}, u32[]{:S(2)}, u32[]{:S(2)}) %collective-permute-start.23) | collective-permute-done | bytes 221216 | tf_op jit(solution)/shard_map/ppermute | solution.py:21
  127.5 1.6 %merge_project.1 = bf16[144,1280]{1,0:T(8,128)(2,1)S(1)} custom-call(bf16[144,768]{1,0:T(8,128)(2,1)S(1)} %get-tuple-element.79.refs_0_, bf16[144,768]{1,0:T(8,128)(2,1)S(1)} %collective-permute-done.21.refs_1_, bf16[144,768]{1,0:T(8,128)(2,1)S(1)} %collective-permute-done.22.refs_2_, bf16[144,768]{1,0:T(8,128)(2,1)S(1)} %collective-permute-done.23.refs_3_, ...), custom_call_target="tpu_custom_call" | custom-call | flops 235929600 | bytes 1638400 | tf_op jit(solution)/shard_map/merge_project/pallas_call | solution.py:219
  129.2 11.8 %collective-permute-start.24 = (bf16[72,1280]{1,0:T(8,128)(2,1)S(1)}, bf16[72,1280]{1,0:T(8,128)(2,1)S(1)}, u32[]{:S(2)}, u32[]{:S(2)}) collective-permute-start(bf16[72,1280]{1,0:T(8,128)(2,1)S(1)} %dynamic-slice_bitcast_fusion), channel_id=1, source_target_pairs={{0,1},{1,0},{2,3},{3,2},{4,5},{5,4},{6,7},{7,6},{8,9},{9,8},{10,11... | collective-permute-start | bytes 552968 | tf_op jit(solution)/shard_map/ppermute | solution.py:21
  (44 shorter events, 8.1 us)
Async XLA Ops:
  0.0 80.8 %copy-start.2 = (bf16[144,640]{1,0:T(8,128)(2,1)S(1)}, bf16[144,640]{1,0:T(8,128)(2,1)}, u32[]{:S(2)}) copy-start(bf16[144,640]{1,0:T(8,128)(2,1)} %refs_1_.1) | copy-start | bytes 552964
  0.0 80.8 %copy-start.1 = (bf16[144,640]{1,0:T(8,128)(2,1)S(1)}, bf16[144,640]{1,0:T(8,128)(2,1)}, u32[]{:S(2)}) copy-start(bf16[144,640]{1,0:T(8,128)(2,1)} %refs_2_.1) | copy-start | bytes 552964
  0.0 27.6 %collective-permute-start.3 = (bf16[144,640]{1,0:T(8,128)(2,1)}, bf16[144,640]{1,0:T(8,128)(2,1)S(1)}, u32[]{:S(2)}, u32[]{:S(2)}) collective-permute-start(bf16[144,640]{1,0:T(8,128)(2,1)} %refs_1_.1), channel_id=1, source_target_pairs={{0,8},{8,16},{16,24},{24,32},{32,40},{40,48},{48,56},{56,64},{64,7... | collective-permute-start | bytes 552968 | tf_op jit(solution)/shard_map/ppermute | solution.py:21
  3.3 28.2 %collective-permute-start.4 = (bf16[144,640]{1,0:T(8,128)(2,1)}, bf16[144,640]{1,0:T(8,128)(2,1)S(1)}, u32[]{:S(2)}, u32[]{:S(2)}) collective-permute-start(bf16[144,640]{1,0:T(8,128)(2,1)} %refs_2_.1), channel_id=1, source_target_pairs={{0,8},{8,16},{16,24},{24,32},{32,40},{40,48},{48,56},{56,64},{64,7... | collective-permute-start | bytes 552968 | tf_op jit(solution)/shard_map/ppermute | solution.py:21
  5.8 25.8 %collective-permute-start.5 = (bf16[144,640]{1,0:T(8,128)(2,1)}, bf16[144,640]{1,0:T(8,128)(2,1)S(1)}, u32[]{:S(2)}, u32[]{:S(2)}) collective-permute-start(bf16[144,640]{1,0:T(8,128)(2,1)} %refs_1_.1), channel_id=1, source_target_pairs={{0,120},{8,0},{16,8},{24,16},{32,24},{40,32},{48,40},{56,48},{64,5... | collective-permute-start | bytes 552968 | tf_op jit(solution)/shard_map/ppermute | solution.py:21
  23.2 8.4 %collective-permute-start.6 = (bf16[144,640]{1,0:T(8,128)(2,1)}, bf16[144,640]{1,0:T(8,128)(2,1)S(1)}, u32[]{:S(2)}, u32[]{:S(2)}) collective-permute-start(bf16[144,640]{1,0:T(8,128)(2,1)} %refs_2_.1), channel_id=1, source_target_pairs={{0,120},{8,0},{16,8},{24,16},{32,24},{40,32},{48,40},{56,48},{64,5... | collective-permute-start | bytes 552968 | tf_op jit(solution)/shard_map/ppermute | solution.py:21
  31.7 10.3 %collective-permute-start.7 = (bf16[288,640]{1,0:T(8,128)(2,1)S(1)}, bf16[288,640]{1,0:T(8,128)(2,1)S(1)}, u32[]{:S(2)}, u32[]{:S(2)}) collective-permute-start(bf16[288,640]{1,0:T(8,128)(2,1)S(1)} %pad_maximum_fusion.refs_3_), channel_id=1, source_target_pairs={{0,8},{8,16},{16,24},{24,32},{32,40},{40,48},{48,56},{56,64},{64,7... | collective-permute-start | bytes 1105928 | tf_op jit(solution)/shard_map/ppermute | solution.py:21
  31.8 10.1 %collective-permute-start.8 = (bf16[288,640]{1,0:T(8,128)(2,1)S(1)}, bf16[288,640]{1,0:T(8,128)(2,1)S(1)}, u32[]{:S(2)}, u32[]{:S(2)}) collective-permute-start(bf16[288,640]{1,0:T(8,128)(2,1)S(1)} %pad_maximum_fusion.1.refs_4_), channel_id=1, source_target_pairs={{0,120},{8,0},{16,8},{24,16},{32,24},{40,32},{48,40},{56,48},{64,5... | collective-permute-start | bytes 1105928 | tf_op jit(solution)/shard_map/ppermute | solution.py:21
  41.9 8.1 %collective-permute-start.10 = (bf16[288,640]{1,0:T(8,128)(2,1)S(1)}, bf16[288,640]{1,0:T(8,128)(2,1)S(1)}, u32[]{:S(2)}, u32[]{:S(2)}) collective-permute-start(bf16[288,640]{1,0:T(8,128)(2,1)S(1)} %collective-permute-done.8.refs_2_), channel_id=1, source_target_pairs={{0,120},{8,0},{16,8},{24,16},{32,24},{40,32},{48,40},{56,48},{64,5... | collective-permute-start | bytes 1105928 | tf_op jit(solution)/shard_map/ppermute | solution.py:21
  44.3 8.8 %collective-permute-start.9 = (bf16[288,640]{1,0:T(8,128)(2,1)S(1)}, bf16[288,640]{1,0:T(8,128)(2,1)S(1)}, u32[]{:S(2)}, u32[]{:S(2)}) collective-permute-start(bf16[288,640]{1,0:T(8,128)(2,1)S(1)} %collective-permute-done.7.refs_1_), channel_id=1, source_target_pairs={{0,8},{8,16},{16,24},{24,32},{32,40},{40,48},{48,56},{56,64},{64,7... | collective-permute-start | bytes 1105928 | tf_op jit(solution)/shard_map/ppermute | solution.py:21
  53.1 7.9 %collective-permute-start.11 = (bf16[288,640]{1,0:T(8,128)(2,1)S(1)}, bf16[288,640]{1,0:T(8,128)(2,1)S(1)}, u32[]{:S(2)}, u32[]{:S(2)}) collective-permute-start(bf16[288,640]{1,0:T(8,128)(2,1)S(1)} %collective-permute-done.9.refs_1_), channel_id=1, source_target_pairs={{0,8},{8,16},{16,24},{24,32},{32,40},{40,48},{48,56},{56,64},{64,7... | collective-permute-start | bytes 1105928 | tf_op jit(solution)/shard_map/ppermute | solution.py:21
  53.1 7.9 %collective-permute-start.12 = (bf16[288,640]{1,0:T(8,128)(2,1)S(1)}, bf16[288,640]{1,0:T(8,128)(2,1)S(1)}, u32[]{:S(2)}, u32[]{:S(2)}) collective-permute-start(bf16[288,640]{1,0:T(8,128)(2,1)S(1)} %collective-permute-done.10.refs_2_), channel_id=1, source_target_pairs={{0,120},{8,0},{16,8},{24,16},{32,24},{40,32},{48,40},{56,48},{64,5... | collective-permute-start | bytes 1105928 | tf_op jit(solution)/shard_map/ppermute | solution.py:21
  61.0 7.6 %collective-permute-start.13 = (bf16[288,640]{1,0:T(8,128)(2,1)S(1)}, bf16[288,640]{1,0:T(8,128)(2,1)S(1)}, u32[]{:S(2)}, u32[]{:S(2)}) collective-permute-start(bf16[288,640]{1,0:T(8,128)(2,1)S(1)} %collective-permute-done.11.refs_1_), channel_id=1, source_target_pairs={{0,8},{8,16},{16,24},{24,32},{32,40},{40,48},{48,56},{56,64},{64,7... | collective-permute-start | bytes 1105928 | tf_op jit(solution)/shard_map/ppermute | solution.py:21
  61.0 7.6 %collective-permute-start.14 = (bf16[288,640]{1,0:T(8,128)(2,1)S(1)}, bf16[288,640]{1,0:T(8,128)(2,1)S(1)}, u32[]{:S(2)}, u32[]{:S(2)}) collective-permute-start(bf16[288,640]{1,0:T(8,128)(2,1)S(1)} %collective-permute-done.12.refs_2_), channel_id=1, source_target_pairs={{0,120},{8,0},{16,8},{24,16},{32,24},{40,32},{48,40},{56,48},{64,5... | collective-permute-start | bytes 1105928 | tf_op jit(solution)/shard_map/ppermute | solution.py:21
  68.6 9.0 %collective-permute-start.15 = (bf16[288,640]{1,0:T(8,128)(2,1)S(1)}, bf16[288,640]{1,0:T(8,128)(2,1)S(1)}, u32[]{:S(2)}, u32[]{:S(2)}) collective-permute-start(bf16[288,640]{1,0:T(8,128)(2,1)S(1)} %collective-permute-done.13.refs_1_), channel_id=1, source_target_pairs={{0,8},{8,16},{16,24},{24,32},{32,40},{40,48},{48,56},{56,64},{64,7... | collective-permute-start | bytes 1105928 | tf_op jit(solution)/shard_map/ppermute | solution.py:21
  68.6 9.0 %collective-permute-start.16 = (bf16[288,640]{1,0:T(8,128)(2,1)S(1)}, bf16[288,640]{1,0:T(8,128)(2,1)S(1)}, u32[]{:S(2)}, u32[]{:S(2)}) collective-permute-start(bf16[288,640]{1,0:T(8,128)(2,1)S(1)} %collective-permute-done.14.refs_2_), channel_id=1, source_target_pairs={{0,120},{8,0},{16,8},{24,16},{32,24},{40,32},{48,40},{56,48},{64,5... | collective-permute-start | bytes 1105928 | tf_op jit(solution)/shard_map/ppermute | solution.py:21
  71.5 6.1 %collective-permute-start = (bf16[144,640]{1,0:T(8,128)(2,1)}, bf16[144,640]{1,0:T(8,128)(2,1)S(1)}, u32[]{:S(2)}, u32[]{:S(2)}) collective-permute-start(bf16[144,640]{1,0:T(8,128)(2,1)} %param.4), channel_id=1, source_target_pairs={{0,2},{2,4},{4,6},{6,0},{1,3},{3,5},{5,7},{7,1},{8,10},{10,12},{12... | collective-permute-start | bytes 552968 | tf_op jit(solution)/shard_map/ppermute | solution.py:21
  72.8 7.8 %collective-permute-start.1 = (bf16[144,640]{1,0:T(8,128)(2,1)}, bf16[144,640]{1,0:T(8,128)(2,1)S(1)}, u32[]{:S(2)}, u32[]{:S(2)}) collective-permute-start(bf16[144,640]{1,0:T(8,128)(2,1)} %param.4), channel_id=1, source_target_pairs={{0,4},{2,6},{4,0},{6,2},{1,5},{3,7},{5,1},{7,3},{8,12},{10,14},{12... | collective-permute-start | bytes 552968 | tf_op jit(solution)/shard_map/ppermute | solution.py:21
  75.6 5.1 %collective-permute-start.2 = (bf16[144,640]{1,0:T(8,128)(2,1)}, bf16[144,640]{1,0:T(8,128)(2,1)S(1)}, u32[]{:S(2)}, u32[]{:S(2)}) collective-permute-start(bf16[144,640]{1,0:T(8,128)(2,1)} %param.4), channel_id=1, source_target_pairs={{0,6},{2,0},{4,2},{6,4},{1,7},{3,1},{5,3},{7,5},{8,14},{10,8},{12,... | collective-permute-start | bytes 552968 | tf_op jit(solution)/shard_map/ppermute | solution.py:21
  77.6 12.2 %collective-permute-start.17 = (bf16[288,640]{1,0:T(8,128)(2,1)S(1)}, bf16[288,640]{1,0:T(8,128)(2,1)S(1)}, u32[]{:S(2)}, u32[]{:S(2)}) collective-permute-start(bf16[288,640]{1,0:T(8,128)(2,1)S(1)} %collective-permute-done.15.refs_1_), channel_id=1, source_target_pairs={{0,8},{8,16},{16,24},{24,32},{32,40},{40,48},{48,56},{56,64},{64,7... | collective-permute-start | bytes 1105928 | tf_op jit(solution)/shard_map/ppermute | solution.py:21
  77.8 12.1 %collective-permute-start.18 = (bf16[288,640]{1,0:T(8,128)(2,1)S(1)}, bf16[288,640]{1,0:T(8,128)(2,1)S(1)}, u32[]{:S(2)}, u32[]{:S(2)}) collective-permute-start(bf16[288,640]{1,0:T(8,128)(2,1)S(1)} %collective-permute-done.16.refs_2_), channel_id=1, source_target_pairs={{0,120},{8,0},{16,8},{24,16},{32,24},{40,32},{48,40},{56,48},{64,5... | collective-permute-start | bytes 1105928 | tf_op jit(solution)/shard_map/ppermute | solution.py:21
  89.9 23.3 %collective-permute-start.19 = (bf16[144,640]{1,0:T(8,128)(2,1)S(1)}, bf16[144,640]{1,0:T(8,128)(2,1)S(1)}, u32[]{:S(2)}, u32[]{:S(2)}) collective-permute-start(bf16[144,640]{1,0:T(8,128)(2,1)S(1)} %slice.6), channel_id=1, source_target_pairs={{0,8},{8,16},{16,24},{24,32},{32,40},{40,48},{48,56},{56,64},{64,7... | collective-permute-start | bytes 552968 | tf_op jit(solution)/shard_map/ppermute | solution.py:21
  90.0 23.1 %collective-permute-start.20 = (bf16[144,640]{1,0:T(8,128)(2,1)S(1)}, bf16[144,640]{1,0:T(8,128)(2,1)S(1)}, u32[]{:S(2)}, u32[]{:S(2)}) collective-permute-start(bf16[144,640]{1,0:T(8,128)(2,1)S(1)} %slice.7), channel_id=1, source_target_pairs={{0,120},{8,0},{16,8},{24,16},{32,24},{40,32},{48,40},{56,48},{64,5... | collective-permute-start | bytes 552968 | tf_op jit(solution)/shard_map/ppermute | solution.py:21
  113.1 14.4 %copy-start = (bf16[640,1280]{1,0:T(8,128)(2,1)S(1)}, bf16[640,1280]{1,0:T(8,128)(2,1)}, u32[]{:S(2)}) copy-start(bf16[640,1280]{1,0:T(8,128)(2,1)} %refs_4_.1) | copy-start | bytes 4915204
  116.2 7.9 %collective-permute-start.21 = (bf16[144,768]{1,0:T(8,128)(2,1)S(1)}, bf16[144,768]{1,0:T(8,128)(2,1)S(1)}, u32[]{:S(2)}, u32[]{:S(2)}) collective-permute-start(bf16[144,768]{1,0:T(8,128)(2,1)S(1)} %get-tuple-element.80), channel_id=1, source_target_pairs={{0,6},{2,0},{4,2},{6,4},{1,7},{3,1},{5,3},{7,5},{8,14},{10,8},{12,... | collective-permute-start | bytes 663560 | tf_op jit(solution)/shard_map/ppermute | solution.py:21
  118.9 6.4 %collective-permute-start.22 = (bf16[144,768]{1,0:T(8,128)(2,1)S(1)}, bf16[144,768]{1,0:T(8,128)(2,1)S(1)}, u32[]{:S(2)}, u32[]{:S(2)}) collective-permute-start(bf16[144,768]{1,0:T(8,128)(2,1)S(1)} %get-tuple-element.81), channel_id=1, source_target_pairs={{0,4},{2,6},{4,0},{6,2},{1,5},{3,7},{5,1},{7,3},{8,12},{10,14},{12... | collective-permute-start | bytes 663560 | tf_op jit(solution)/shard_map/ppermute | solution.py:21
  119.2 8.4 %collective-permute-start.23 = (bf16[144,768]{1,0:T(8,128)(2,1)S(1)}, bf16[144,768]{1,0:T(8,128)(2,1)S(1)}, u32[]{:S(2)}, u32[]{:S(2)}) collective-permute-start(bf16[144,768]{1,0:T(8,128)(2,1)S(1)} %get-tuple-element.82), channel_id=1, source_target_pairs={{0,2},{2,4},{4,6},{6,0},{1,3},{3,5},{5,7},{7,1},{8,10},{10,12},{12... | collective-permute-start | bytes 663560 | tf_op jit(solution)/shard_map/ppermute | solution.py:21
  129.2 12.9 %collective-permute-start.24 = (bf16[72,1280]{1,0:T(8,128)(2,1)S(1)}, bf16[72,1280]{1,0:T(8,128)(2,1)S(1)}, u32[]{:S(2)}, u32[]{:S(2)}) collective-permute-start(bf16[72,1280]{1,0:T(8,128)(2,1)S(1)} %dynamic-slice_bitcast_fusion), channel_id=1, source_target_pairs={{0,1},{1,0},{2,3},{3,2},{4,5},{5,4},{6,7},{7,6},{8,9},{9,8},{10,11... | collective-permute-start | bytes 552968 | tf_op jit(solution)/shard_map/ppermute | solution.py:21

commit v2 on v1

--- a/solution.py
+++ b/solution.py
@@ -245,9 +245,6 @@
     state = None
     for turn in range(1, half + 1):
         final = turn == half
-        if turn > 1:
-            up, down = lax.optimization_barrier((up, down))
-            held = held[: len(held) - 2] + [piece(up), piece(down)]
         if final:
             k = shifted(up[:rows], "blk", 1)
             v = shifted(down[rows:], "blk", -1)
@@ -277,7 +274,7 @@
         held = held + arrived
 
     parts = list(attend_step(queries, held, state, True, blocks)[2:])
-    for d in turns:
+    for d in reversed(turns):
         parts[d] = shifted(parts[d], "node", -d)
     mine = merge_project(parts, out_weight)
 

time: 143 us -> 140 us (0.979)
  waiting for transfers between devices: 42.3 us -> 40.4 us
    ppermute x25, waiting for transfers between devices: 42.3 us -> 40.4 us  [shifted(): lax.ppermute(array, axis, [(i, (i + by) % size) for i in range(size)])]
  transfers between devices with their start and end apart: 25 -> 25, of which waited for: 12 -> 11; matrix products, arithmetic and copies ran while one was open for 1% -> 1% of each run, Pallas kernels for 21% -> 21%
where the time goes in v2:
time: 140 us
  starting transfers between devices  62.9 us (45%)
  waiting for transfers between devices  40.4 us (29%)
  Pallas kernels  34 us (24%)
    ppermute x25, starting transfers between devices, shifted(): lax.ppermute(array, axis, [(i, (i + by) % size) for i in range(size)])  62.9 us
    ppermute x25, waiting for transfers between devices, shifted(): lax.ppermute(array, axis, [(i, (i + by) % size) for i in range(size)])  40.4 us
    pallas_call x8, Pallas kernels, attend_step(): pl.pallas_call(body, out_shape=outs, in_specs=[vmem] * inputs, out_specs=...  32.4 us
  transfers between devices with their start and end apart: 25, of which 11 were waited for; matrix products, arithmetic and copies ran while one was open for 1% of the time, Pallas kernels for 21%

profile of v2, /device:TPU:33, one launch (start us, length us, event | category | flops | bytes accessed | tf_op | source)
XLA Modules:
  0.0 139.6 jit_solution(18275020250339095469)
XLA Ops:
  0.0 3.3 %collective-permute-start.3 = (bf16[144,640]{1,0:T(8,128)(2,1)}, bf16[144,640]{1,0:T(8,128)(2,1)S(1)}, u32[]{:S(2)}, u32[]{:S(2)}) collective-permute-start(bf16[144,640]{1,0:T(8,128)(2,1)} %refs_1_.1), channel_id=1, source_target_pairs={{0,8},{8,16},{16,24},{24,32},{32,40},{40,48},{48,56},{56,64},{64,7... | collective-permute-start | bytes 552968 | tf_op jit(solution)/shard_map/ppermute | solution.py:21
  3.3 2.5 %collective-permute-start.4 = (bf16[144,640]{1,0:T(8,128)(2,1)}, bf16[144,640]{1,0:T(8,128)(2,1)S(1)}, u32[]{:S(2)}, u32[]{:S(2)}) collective-permute-start(bf16[144,640]{1,0:T(8,128)(2,1)} %refs_2_.1), channel_id=1, source_target_pairs={{0,8},{8,16},{16,24},{24,32},{32,40},{40,48},{48,56},{56,64},{64,7... | collective-permute-start | bytes 552968 | tf_op jit(solution)/shard_map/ppermute | solution.py:21
  5.8 17.4 %collective-permute-start.12 = (bf16[144,640]{1,0:T(8,128)(2,1)}, bf16[144,640]{1,0:T(8,128)(2,1)S(1)}, u32[]{:S(2)}, u32[]{:S(2)}) collective-permute-start(bf16[144,640]{1,0:T(8,128)(2,1)} %refs_1_.1), channel_id=1, source_target_pairs={{0,120},{8,0},{16,8},{24,16},{32,24},{40,32},{48,40},{56,48},{64,5... | collective-permute-start | bytes 552968 | tf_op jit(solution)/shard_map/ppermute | solution.py:21
  23.2 1.3 collective-permute-start.13
  24.5 3.1 %collective-permute-done.3 = bf16[144,640]{1,0:T(8,128)(2,1)S(1)} collective-permute-done((bf16[144,640]{1,0:T(8,128)(2,1)}, bf16[144,640]{1,0:T(8,128)(2,1)S(1)}, u32[]{:S(2)}, u32[]{:S(2)}) %collective-permute-start.3) | collective-permute-done | bytes 184352 | tf_op jit(solution)/shard_map/ppermute | solution.py:21
  27.6 3.9 %collective-permute-done.4 = bf16[144,640]{1,0:T(8,128)(2,1)S(1)} collective-permute-done((bf16[144,640]{1,0:T(8,128)(2,1)}, bf16[144,640]{1,0:T(8,128)(2,1)S(1)}, u32[]{:S(2)}, u32[]{:S(2)}) %collective-permute-start.4) | collective-permute-done | bytes 184352 | tf_op jit(solution)/shard_map/ppermute | solution.py:21
  31.8 2.8 %collective-permute-start.14 = (bf16[288,640]{1,0:T(8,128)(2,1)S(1)}, bf16[288,640]{1,0:T(8,128)(2,1)S(1)}, u32[]{:S(2)}, u32[]{:S(2)}) collective-permute-start(bf16[288,640]{1,0:T(8,128)(2,1)S(1)} %constant_dynamic-update-slice_fusion.6.refs_4_), channel_id=1, source_target_pairs={{0,120},{8,0},{16,8},{24,16},{32,24},{40,32},{48,40},{56,48},{64,5... | collective-permute-start | bytes 1105928 | tf_op jit(solution)/shard_map/ppermute | solution.py:21
  34.6 7.3 %collective-permute-done.5.refs_1_ = bf16[288,640]{1,0:T(8,128)(2,1)S(1)} collective-permute-done((bf16[288,640]{1,0:T(8,128)(2,1)S(1)}, bf16[288,640]{1,0:T(8,128)(2,1)S(1)}, u32[]{:S(2)}, u32[]{:S(2)}) %collective-permute-start.5) | collective-permute-done | bytes 368672 | tf_op jit(solution)/shard_map/ppermute | solution.py:21
  41.9 2.7 %collective-permute-start.15 = (bf16[288,640]{1,0:T(8,128)(2,1)S(1)}, bf16[288,640]{1,0:T(8,128)(2,1)S(1)}, u32[]{:S(2)}, u32[]{:S(2)}) collective-permute-start(bf16[288,640]{1,0:T(8,128)(2,1)S(1)} %collective-permute-done.14.refs_2_), channel_id=1, source_target_pairs={{0,120},{8,0},{16,8},{24,16},{32,24},{40,32},{48,40},{56,48},{64,5... | collective-permute-start | bytes 1105928 | tf_op jit(solution)/shard_map/ppermute | solution.py:21
  44.6 6.6 %collective-permute-done.6.refs_1_ = bf16[288,640]{1,0:T(8,128)(2,1)S(1)} collective-permute-done((bf16[288,640]{1,0:T(8,128)(2,1)S(1)}, bf16[288,640]{1,0:T(8,128)(2,1)S(1)}, u32[]{:S(2)}, u32[]{:S(2)}) %collective-permute-start.6) | collective-permute-done | bytes 368672 | tf_op jit(solution)/shard_map/ppermute | solution.py:21
  51.2 2.7 %collective-permute-start.16 = (bf16[288,640]{1,0:T(8,128)(2,1)S(1)}, bf16[288,640]{1,0:T(8,128)(2,1)S(1)}, u32[]{:S(2)}, u32[]{:S(2)}) collective-permute-start(bf16[288,640]{1,0:T(8,128)(2,1)S(1)} %collective-permute-done.15.refs_2_), channel_id=1, source_target_pairs={{0,120},{8,0},{16,8},{24,16},{32,24},{40,32},{48,40},{56,48},{64,5... | collective-permute-start | bytes 1105928 | tf_op jit(solution)/shard_map/ppermute | solution.py:21
  53.9 5.8 %collective-permute-done.7.refs_1_ = bf16[288,640]{1,0:T(8,128)(2,1)S(1)} collective-permute-done((bf16[288,640]{1,0:T(8,128)(2,1)S(1)}, bf16[288,640]{1,0:T(8,128)(2,1)S(1)}, u32[]{:S(2)}, u32[]{:S(2)}) %collective-permute-start.7) | collective-permute-done | bytes 368672 | tf_op jit(solution)/shard_map/ppermute | solution.py:21
  59.7 2.7 %collective-permute-start.17 = (bf16[288,640]{1,0:T(8,128)(2,1)S(1)}, bf16[288,640]{1,0:T(8,128)(2,1)S(1)}, u32[]{:S(2)}, u32[]{:S(2)}) collective-permute-start(bf16[288,640]{1,0:T(8,128)(2,1)S(1)} %collective-permute-done.16.refs_2_), channel_id=1, source_target_pairs={{0,120},{8,0},{16,8},{24,16},{32,24},{40,32},{48,40},{56,48},{64,5... | collective-permute-start | bytes 1105928 | tf_op jit(solution)/shard_map/ppermute | solution.py:21
  62.3 4.9 %collective-permute-done.8.refs_1_ = bf16[288,640]{1,0:T(8,128)(2,1)S(1)} collective-permute-done((bf16[288,640]{1,0:T(8,128)(2,1)S(1)}, bf16[288,640]{1,0:T(8,128)(2,1)S(1)}, u32[]{:S(2)}, u32[]{:S(2)}) %collective-permute-start.8) | collective-permute-done | bytes 368672 | tf_op jit(solution)/shard_map/ppermute | solution.py:21
  67.2 2.7 %collective-permute-start.18 = (bf16[288,640]{1,0:T(8,128)(2,1)S(1)}, bf16[288,640]{1,0:T(8,128)(2,1)S(1)}, u32[]{:S(2)}, u32[]{:S(2)}) collective-permute-start(bf16[288,640]{1,0:T(8,128)(2,1)S(1)} %collective-permute-done.17.refs_2_), channel_id=1, source_target_pairs={{0,120},{8,0},{16,8},{24,16},{32,24},{40,32},{48,40},{56,48},{64,5... | collective-permute-start | bytes 1105928 | tf_op jit(solution)/shard_map/ppermute | solution.py:21
  69.9 1.3 collective-permute-start
  71.3 2.7 %collective-permute-start.1 = (bf16[144,640]{1,0:T(8,128)(2,1)}, bf16[144,640]{1,0:T(8,128)(2,1)S(1)}, u32[]{:S(2)}, u32[]{:S(2)}) collective-permute-start(bf16[144,640]{1,0:T(8,128)(2,1)} %param.4), channel_id=1, source_target_pairs={{0,4},{2,6},{4,0},{6,2},{1,5},{3,7},{5,1},{7,3},{8,12},{10,14},{12... | collective-permute-start | bytes 552968 | tf_op jit(solution)/shard_map/ppermute | solution.py:21
  76.2 2.6 %collective-permute-start.19 = (bf16[288,640]{1,0:T(8,128)(2,1)S(1)}, bf16[288,640]{1,0:T(8,128)(2,1)S(1)}, u32[]{:S(2)}, u32[]{:S(2)}) collective-permute-start(bf16[288,640]{1,0:T(8,128)(2,1)S(1)} %collective-permute-done.18.refs_2_), channel_id=1, source_target_pairs={{0,120},{8,0},{16,8},{24,16},{32,24},{40,32},{48,40},{56,48},{64,5... | collective-permute-start | bytes 1105928 | tf_op jit(solution)/shard_map/ppermute | solution.py:21
  79.2 4.9 %attend.8 = (f32[16,640]{1,0:T(8,128)S(1)}, f32[16,640]{1,0:T(8,128)S(1)}, f32[704,640]{1,0:T(8,128)S(1)}) custom-call(bf16[640,640]{1,0:T(8,128)(2,1)S(1)} %broadcast_dynamic-update-slice_fusion.refs_0_, bf16[144,640]{1,0:T(8,128)(2,1)S(1)} %copy-done.1, bf16[144,640]{1,0:T(8,128)(2,1)S(1)} %copy-done.2, ...), custom_call_target="tpu_custom_call" | custom-call | flops 707788800 | bytes 1638400 | tf_op jit(solution)/shard_map/attend/pallas_call | solution.py:160
  84.1 4.1 %attend.9 = (f32[16,640]{1,0:T(8,128)S(1)}, f32[16,640]{1,0:T(8,128)S(1)}, f32[704,640]{1,0:T(8,128)S(1)}) custom-call(bf16[640,640]{1,0:T(8,128)(2,1)S(1)} %broadcast_dynamic-update-slice_fusion.refs_0_, bf16[288,640]{1,0:T(8,128)(2,1)S(1)} %collective-permute-done.5.refs_1_, ...), custom_call_target="tpu_custom_call", output_to_operand_aliasing={{0}: (3, {}), {1}: (4, {}), {2}: (5, {})} | custom-call | flops 471859200 | bytes 1638400 | tf_op jit(solution)/shard_map/attend/pallas_call | solution.py:160
  88.4 2.8 %collective-permute-start.20 = (bf16[144,640]{1,0:T(8,128)(2,1)S(1)}, bf16[144,640]{1,0:T(8,128)(2,1)S(1)}, u32[]{:S(2)}, u32[]{:S(2)}) collective-permute-start(bf16[144,640]{1,0:T(8,128)(2,1)S(1)} %slice.9), channel_id=1, source_target_pairs={{0,120},{8,0},{16,8},{24,16},{32,24},{40,32},{48,40},{56,48},{64,5... | collective-permute-start | bytes 552968 | tf_op jit(solution)/shard_map/ppermute | solution.py:21
  91.2 4.1 %attend.10 = (f32[16,640]{1,0:T(8,128)S(1)}, f32[16,640]{1,0:T(8,128)S(1)}, f32[704,640]{1,0:T(8,128)S(1)}) custom-call(bf16[640,640]{1,0:T(8,128)(2,1)S(1)} %broadcast_dynamic-update-slice_fusion.refs_0_, bf16[288,640]{1,0:T(8,128)(2,1)S(1)} %collective-permute-done.6.refs_1_, ...), custom_call_target="tpu_custom_call", output_to_operand_aliasing={{0}: (3, {}), {1}: (4, {}), {2}: (5, {})} | custom-call | flops 471859200 | bytes 1638400 | tf_op jit(solution)/shard_map/attend/pallas_call | solution.py:160
  95.2 4.1 %attend.11 = (f32[16,640]{1,0:T(8,128)S(1)}, f32[16,640]{1,0:T(8,128)S(1)}, f32[704,640]{1,0:T(8,128)S(1)}) custom-call(bf16[640,640]{1,0:T(8,128)(2,1)S(1)} %broadcast_dynamic-update-slice_fusion.refs_0_, bf16[288,640]{1,0:T(8,128)(2,1)S(1)} %collective-permute-done.7.refs_1_, ...), custom_call_target="tpu_custom_call", output_to_operand_aliasing={{0}: (3, {}), {1}: (4, {}), {2}: (5, {})} | custom-call | flops 471859200 | bytes 1638400 | tf_op jit(solution)/shard_map/attend/pallas_call | solution.py:160
  99.3 4.1 %attend.12 = (f32[16,640]{1,0:T(8,128)S(1)}, f32[16,640]{1,0:T(8,128)S(1)}, f32[704,640]{1,0:T(8,128)S(1)}) custom-call(bf16[640,640]{1,0:T(8,128)(2,1)S(1)} %broadcast_dynamic-update-slice_fusion.refs_0_, bf16[288,640]{1,0:T(8,128)(2,1)S(1)} %collective-permute-done.8.refs_1_, ...), custom_call_target="tpu_custom_call", output_to_operand_aliasing={{0}: (3, {}), {1}: (4, {}), {2}: (5, {})} | custom-call | flops 471859200 | bytes 1638400 | tf_op jit(solution)/shard_map/attend/pallas_call | solution.py:160
  103.4 4.1 %attend.13 = (f32[16,640]{1,0:T(8,128)S(1)}, f32[16,640]{1,0:T(8,128)S(1)}, f32[704,640]{1,0:T(8,128)S(1)}) custom-call(bf16[640,640]{1,0:T(8,128)(2,1)S(1)} %broadcast_dynamic-update-slice_fusion.refs_0_, bf16[288,640]{1,0:T(8,128)(2,1)S(1)} %collective-permute-done.9.refs_1_, ...), custom_call_target="tpu_custom_call", output_to_operand_aliasing={{0}: (3, {}), {1}: (4, {}), {2}: (5, {})} | custom-call | flops 471859200 | bytes 1638400 | tf_op jit(solution)/shard_map/attend/pallas_call | solution.py:160
  107.4 4.1 %attend.14 = (f32[16,640]{1,0:T(8,128)S(1)}, f32[16,640]{1,0:T(8,128)S(1)}, f32[704,640]{1,0:T(8,128)S(1)}) custom-call(bf16[640,640]{1,0:T(8,128)(2,1)S(1)} %broadcast_dynamic-update-slice_fusion.refs_0_, bf16[288,640]{1,0:T(8,128)(2,1)S(1)} %collective-permute-done.10.refs_1_, ...), custom_call_target="tpu_custom_call", output_to_operand_aliasing={{0}: (3, {}), {1}: (4, {}), {2}: (5, {})} | custom-call | flops 471859200 | bytes 1638400 | tf_op jit(solution)/shard_map/attend/pallas_call | solution.py:160
  111.5 3.1 %attend.15 = (f32[16,640]{1,0:T(8,128)}, f32[16,640]{1,0:T(8,128)}, bf16[144,768]{1,0:T(8,128)(2,1)S(1)}, bf16[144,768]{1,0:T(8,128)(2,1)S(1)}, bf16[144,768]{1,...) custom-call(bf16[640,640]{1,0:T(8,128)(2,1)S(1)} %broadcast_dynamic-update-slice_fusion.refs_0_, ...), custom_call_target="tpu_custom_call" | custom-call | flops 235929600 | bytes 1638400 | tf_op jit(solution)/shard_map/attend/pallas_call | solution.py:160
  114.6 2.2 %collective-permute-start.21 = (bf16[144,768]{1,0:T(8,128)(2,1)S(1)}, bf16[144,768]{1,0:T(8,128)(2,1)S(1)}, u32[]{:S(2)}, u32[]{:S(2)}) collective-permute-start(bf16[144,768]{1,0:T(8,128)(2,1)S(1)} %get-tuple-element.52), channel_id=1, source_target_pairs={{0,6},{2,0},{4,2},{6,4},{1,7},{3,1},{5,3},{7,5},{8,14},{10,8},{12,... | collective-permute-start | bytes 663560 | tf_op jit(solution)/shard_map/ppermute | solution.py:21
  118.0 4.0 %collective-permute-done.21.refs_1_ = bf16[144,768]{1,0:T(8,128)(2,1)S(1)} collective-permute-done((bf16[144,768]{1,0:T(8,128)(2,1)S(1)}, bf16[144,768]{1,0:T(8,128)(2,1)S(1)}, u32[]{:S(2)}, u32[]{:S(2)}) %collective-permute-start.21) | collective-permute-done | bytes 221216 | tf_op jit(solution)/shard_map/ppermute | solution.py:21
  123.2 2.3 %collective-permute-done.23.refs_3_ = bf16[144,768]{1,0:T(8,128)(2,1)S(1)} collective-permute-done((bf16[144,768]{1,0:T(8,128)(2,1)S(1)}, bf16[144,768]{1,0:T(8,128)(2,1)S(1)}, u32[]{:S(2)}, u32[]{:S(2)}) %collective-permute-start.23) | collective-permute-done | bytes 221216 | tf_op jit(solution)/shard_map/ppermute | solution.py:21
  125.5 1.6 %merge_project.1 = bf16[144,1280]{1,0:T(8,128)(2,1)S(1)} custom-call(bf16[144,768]{1,0:T(8,128)(2,1)S(1)} %get-tuple-element.51.refs_0_, bf16[144,768]{1,0:T(8,128)(2,1)S(1)} %collective-permute-done.21.refs_1_, bf16[144,768]{1,0:T(8,128)(2,1)S(1)} %collective-permute-done.22.refs_2_, bf16[144,768]{1,0:T(8,128)(2,1)S(1)} %collective-permute-done.23.refs_3_, ...), custom_call_target="tpu_custom_call" | custom-call | flops 235929600 | bytes 1638400 | tf_op jit(solution)/shard_map/merge_project/pallas_call | solution.py:219
  127.1 10.7 %collective-permute-start.24 = (bf16[72,1280]{1,0:T(8,128)(2,1)S(1)}, bf16[72,1280]{1,0:T(8,128)(2,1)S(1)}, u32[]{:S(2)}, u32[]{:S(2)}) collective-permute-start(bf16[72,1280]{1,0:T(8,128)(2,1)S(1)} %dynamic-slice_bitcast_fusion), channel_id=1, source_target_pairs={{0,1},{1,0},{2,3},{3,2},{4,5},{5,4},{6,7},{7,6},{8,9},{9,8},{10,11... | collective-permute-start | bytes 552968 | tf_op jit(solution)/shard_map/ppermute | solution.py:21
  (46 shorter events, 7.1 us)
Async XLA Ops:
  0.0 79.2 %copy-start.1 = (bf16[144,640]{1,0:T(8,128)(2,1)S(1)}, bf16[144,640]{1,0:T(8,128)(2,1)}, u32[]{:S(2)}) copy-start(bf16[144,640]{1,0:T(8,128)(2,1)} %refs_1_.1) | copy-start | bytes 552964
  0.0 79.2 %copy-start.2 = (bf16[144,640]{1,0:T(8,128)(2,1)S(1)}, bf16[144,640]{1,0:T(8,128)(2,1)}, u32[]{:S(2)}) copy-start(bf16[144,640]{1,0:T(8,128)(2,1)} %refs_2_.1) | copy-start | bytes 552964
  0.0 27.6 %collective-permute-start.3 = (bf16[144,640]{1,0:T(8,128)(2,1)}, bf16[144,640]{1,0:T(8,128)(2,1)S(1)}, u32[]{:S(2)}, u32[]{:S(2)}) collective-permute-start(bf16[144,640]{1,0:T(8,128)(2,1)} %refs_1_.1), channel_id=1, source_target_pairs={{0,8},{8,16},{16,24},{24,32},{32,40},{40,48},{48,56},{56,64},{64,7... | collective-permute-start | bytes 552968 | tf_op jit(solution)/shard_map/ppermute | solution.py:21
  3.3 28.2 %collective-permute-start.4 = (bf16[144,640]{1,0:T(8,128)(2,1)}, bf16[144,640]{1,0:T(8,128)(2,1)S(1)}, u32[]{:S(2)}, u32[]{:S(2)}) collective-permute-start(bf16[144,640]{1,0:T(8,128)(2,1)} %refs_2_.1), channel_id=1, source_target_pairs={{0,8},{8,16},{16,24},{24,32},{32,40},{40,48},{48,56},{56,64},{64,7... | collective-permute-start | bytes 552968 | tf_op jit(solution)/shard_map/ppermute | solution.py:21
  5.8 25.9 %collective-permute-start.12 = (bf16[144,640]{1,0:T(8,128)(2,1)}, bf16[144,640]{1,0:T(8,128)(2,1)S(1)}, u32[]{:S(2)}, u32[]{:S(2)}) collective-permute-start(bf16[144,640]{1,0:T(8,128)(2,1)} %refs_1_.1), channel_id=1, source_target_pairs={{0,120},{8,0},{16,8},{24,16},{32,24},{40,32},{48,40},{56,48},{64,5... | collective-permute-start | bytes 552968 | tf_op jit(solution)/shard_map/ppermute | solution.py:21
  23.2 8.6 %collective-permute-start.13 = (bf16[144,640]{1,0:T(8,128)(2,1)}, bf16[144,640]{1,0:T(8,128)(2,1)S(1)}, u32[]{:S(2)}, u32[]{:S(2)}) collective-permute-start(bf16[144,640]{1,0:T(8,128)(2,1)} %refs_2_.1), channel_id=1, source_target_pairs={{0,120},{8,0},{16,8},{24,16},{32,24},{40,32},{48,40},{56,48},{64,5... | collective-permute-start | bytes 552968 | tf_op jit(solution)/shard_map/ppermute | solution.py:21
  31.6 10.3 %collective-permute-start.5 = (bf16[288,640]{1,0:T(8,128)(2,1)S(1)}, bf16[288,640]{1,0:T(8,128)(2,1)S(1)}, u32[]{:S(2)}, u32[]{:S(2)}) collective-permute-start(bf16[288,640]{1,0:T(8,128)(2,1)S(1)} %constant_dynamic-update-slice_fusion.4.refs_3_), channel_id=1, source_target_pairs={{0,8},{8,16},{16,24},{24,32},{32,40},{40,48},{48,56},{56,64},{64,7... | collective-permute-start | bytes 1105928 | tf_op jit(solution)/shard_map/ppermute | solution.py:21
  31.8 10.1 %collective-permute-start.14 = (bf16[288,640]{1,0:T(8,128)(2,1)S(1)}, bf16[288,640]{1,0:T(8,128)(2,1)S(1)}, u32[]{:S(2)}, u32[]{:S(2)}) collective-permute-start(bf16[288,640]{1,0:T(8,128)(2,1)S(1)} %constant_dynamic-update-slice_fusion.6.refs_4_), channel_id=1, source_target_pairs={{0,120},{8,0},{16,8},{24,16},{32,24},{40,32},{48,40},{56,48},{64,5... | collective-permute-start | bytes 1105928 | tf_op jit(solution)/shard_map/ppermute | solution.py:21
  41.9 9.3 %collective-permute-start.6 = (bf16[288,640]{1,0:T(8,128)(2,1)S(1)}, bf16[288,640]{1,0:T(8,128)(2,1)S(1)}, u32[]{:S(2)}, u32[]{:S(2)}) collective-permute-start(bf16[288,640]{1,0:T(8,128)(2,1)S(1)} %collective-permute-done.5.refs_1_), channel_id=1, source_target_pairs={{0,8},{8,16},{16,24},{24,32},{32,40},{40,48},{48,56},{56,64},{64,7... | collective-permute-start | bytes 1105928 | tf_op jit(solution)/shard_map/ppermute | solution.py:21
  41.9 9.3 %collective-permute-start.15 = (bf16[288,640]{1,0:T(8,128)(2,1)S(1)}, bf16[288,640]{1,0:T(8,128)(2,1)S(1)}, u32[]{:S(2)}, u32[]{:S(2)}) collective-permute-start(bf16[288,640]{1,0:T(8,128)(2,1)S(1)} %collective-permute-done.14.refs_2_), channel_id=1, source_target_pairs={{0,120},{8,0},{16,8},{24,16},{32,24},{40,32},{48,40},{56,48},{64,5... | collective-permute-start | bytes 1105928 | tf_op jit(solution)/shard_map/ppermute | solution.py:21
  51.2 8.5 %collective-permute-start.7 = (bf16[288,640]{1,0:T(8,128)(2,1)S(1)}, bf16[288,640]{1,0:T(8,128)(2,1)S(1)}, u32[]{:S(2)}, u32[]{:S(2)}) collective-permute-start(bf16[288,640]{1,0:T(8,128)(2,1)S(1)} %collective-permute-done.6.refs_1_), channel_id=1, source_target_pairs={{0,8},{8,16},{16,24},{24,32},{32,40},{40,48},{48,56},{56,64},{64,7... | collective-permute-start | bytes 1105928 | tf_op jit(solution)/shard_map/ppermute | solution.py:21
  51.2 8.5 %collective-permute-start.16 = (bf16[288,640]{1,0:T(8,128)(2,1)S(1)}, bf16[288,640]{1,0:T(8,128)(2,1)S(1)}, u32[]{:S(2)}, u32[]{:S(2)}) collective-permute-start(bf16[288,640]{1,0:T(8,128)(2,1)S(1)} %collective-permute-done.15.refs_2_), channel_id=1, source_target_pairs={{0,120},{8,0},{16,8},{24,16},{32,24},{40,32},{48,40},{56,48},{64,5... | collective-permute-start | bytes 1105928 | tf_op jit(solution)/shard_map/ppermute | solution.py:21
  59.6 7.6 %collective-permute-start.8 = (bf16[288,640]{1,0:T(8,128)(2,1)S(1)}, bf16[288,640]{1,0:T(8,128)(2,1)S(1)}, u32[]{:S(2)}, u32[]{:S(2)}) collective-permute-start(bf16[288,640]{1,0:T(8,128)(2,1)S(1)} %collective-permute-done.7.refs_1_), channel_id=1, source_target_pairs={{0,8},{8,16},{16,24},{24,32},{32,40},{40,48},{48,56},{56,64},{64,7... | collective-permute-start | bytes 1105928 | tf_op jit(solution)/shard_map/ppermute | solution.py:21
  59.7 7.6 %collective-permute-start.17 = (bf16[288,640]{1,0:T(8,128)(2,1)S(1)}, bf16[288,640]{1,0:T(8,128)(2,1)S(1)}, u32[]{:S(2)}, u32[]{:S(2)}) collective-permute-start(bf16[288,640]{1,0:T(8,128)(2,1)S(1)} %collective-permute-done.16.refs_2_), channel_id=1, source_target_pairs={{0,120},{8,0},{16,8},{24,16},{32,24},{40,32},{48,40},{56,48},{64,5... | collective-permute-start | bytes 1105928 | tf_op jit(solution)/shard_map/ppermute | solution.py:21
  67.2 8.8 %collective-permute-start.9 = (bf16[288,640]{1,0:T(8,128)(2,1)S(1)}, bf16[288,640]{1,0:T(8,128)(2,1)S(1)}, u32[]{:S(2)}, u32[]{:S(2)}) collective-permute-start(bf16[288,640]{1,0:T(8,128)(2,1)S(1)} %collective-permute-done.8.refs_1_), channel_id=1, source_target_pairs={{0,8},{8,16},{16,24},{24,32},{32,40},{40,48},{48,56},{56,64},{64,7... | collective-permute-start | bytes 1105928 | tf_op jit(solution)/shard_map/ppermute | solution.py:21
  67.2 8.9 %collective-permute-start.18 = (bf16[288,640]{1,0:T(8,128)(2,1)S(1)}, bf16[288,640]{1,0:T(8,128)(2,1)S(1)}, u32[]{:S(2)}, u32[]{:S(2)}) collective-permute-start(bf16[288,640]{1,0:T(8,128)(2,1)S(1)} %collective-permute-done.17.refs_2_), channel_id=1, source_target_pairs={{0,120},{8,0},{16,8},{24,16},{32,24},{40,32},{48,40},{56,48},{64,5... | collective-permute-start | bytes 1105928 | tf_op jit(solution)/shard_map/ppermute | solution.py:21
  69.9 6.1 %collective-permute-start = (bf16[144,640]{1,0:T(8,128)(2,1)}, bf16[144,640]{1,0:T(8,128)(2,1)S(1)}, u32[]{:S(2)}, u32[]{:S(2)}) collective-permute-start(bf16[144,640]{1,0:T(8,128)(2,1)} %param.4), channel_id=1, source_target_pairs={{0,2},{2,4},{4,6},{6,0},{1,3},{3,5},{5,7},{7,1},{8,10},{10,12},{12... | collective-permute-start | bytes 552968 | tf_op jit(solution)/shard_map/ppermute | solution.py:21
  71.3 7.8 %collective-permute-start.1 = (bf16[144,640]{1,0:T(8,128)(2,1)}, bf16[144,640]{1,0:T(8,128)(2,1)S(1)}, u32[]{:S(2)}, u32[]{:S(2)}) collective-permute-start(bf16[144,640]{1,0:T(8,128)(2,1)} %param.4), channel_id=1, source_target_pairs={{0,4},{2,6},{4,0},{6,2},{1,5},{3,7},{5,1},{7,3},{8,12},{10,14},{12... | collective-permute-start | bytes 552968 | tf_op jit(solution)/shard_map/ppermute | solution.py:21
  74.0 5.1 %collective-permute-start.2 = (bf16[144,640]{1,0:T(8,128)(2,1)}, bf16[144,640]{1,0:T(8,128)(2,1)S(1)}, u32[]{:S(2)}, u32[]{:S(2)}) collective-permute-start(bf16[144,640]{1,0:T(8,128)(2,1)} %param.4), channel_id=1, source_target_pairs={{0,6},{2,0},{4,2},{6,4},{1,7},{3,1},{5,3},{7,5},{8,14},{10,8},{12,... | collective-permute-start | bytes 552968 | tf_op jit(solution)/shard_map/ppermute | solution.py:21
  76.0 12.2 %collective-permute-start.10 = (bf16[288,640]{1,0:T(8,128)(2,1)S(1)}, bf16[288,640]{1,0:T(8,128)(2,1)S(1)}, u32[]{:S(2)}, u32[]{:S(2)}) collective-permute-start(bf16[288,640]{1,0:T(8,128)(2,1)S(1)} %collective-permute-done.9.refs_1_), channel_id=1, source_target_pairs={{0,8},{8,16},{16,24},{24,32},{32,40},{40,48},{48,56},{56,64},{64,7... | collective-permute-start | bytes 1105928 | tf_op jit(solution)/shard_map/ppermute | solution.py:21
  76.2 12.2 %collective-permute-start.19 = (bf16[288,640]{1,0:T(8,128)(2,1)S(1)}, bf16[288,640]{1,0:T(8,128)(2,1)S(1)}, u32[]{:S(2)}, u32[]{:S(2)}) collective-permute-start(bf16[288,640]{1,0:T(8,128)(2,1)S(1)} %collective-permute-done.18.refs_2_), channel_id=1, source_target_pairs={{0,120},{8,0},{16,8},{24,16},{32,24},{40,32},{48,40},{56,48},{64,5... | collective-permute-start | bytes 1105928 | tf_op jit(solution)/shard_map/ppermute | solution.py:21
  88.2 23.3 %collective-permute-start.11 = (bf16[144,640]{1,0:T(8,128)(2,1)S(1)}, bf16[144,640]{1,0:T(8,128)(2,1)S(1)}, u32[]{:S(2)}, u32[]{:S(2)}) collective-permute-start(bf16[144,640]{1,0:T(8,128)(2,1)S(1)} %slice.8), channel_id=1, source_target_pairs={{0,8},{8,16},{16,24},{24,32},{32,40},{40,48},{48,56},{56,64},{64,7... | collective-permute-start | bytes 552968 | tf_op jit(solution)/shard_map/ppermute | solution.py:21
  88.4 23.1 %collective-permute-start.20 = (bf16[144,640]{1,0:T(8,128)(2,1)S(1)}, bf16[144,640]{1,0:T(8,128)(2,1)S(1)}, u32[]{:S(2)}, u32[]{:S(2)}) collective-permute-start(bf16[144,640]{1,0:T(8,128)(2,1)S(1)} %slice.9), channel_id=1, source_target_pairs={{0,120},{8,0},{16,8},{24,16},{32,24},{40,32},{48,40},{56,48},{64,5... | collective-permute-start | bytes 552968 | tf_op jit(solution)/shard_map/ppermute | solution.py:21
  111.5 13.9 %copy-start = (bf16[640,1280]{1,0:T(8,128)(2,1)S(1)}, bf16[640,1280]{1,0:T(8,128)(2,1)}, u32[]{:S(2)}) copy-start(bf16[640,1280]{1,0:T(8,128)(2,1)} %refs_4_.1) | copy-start | bytes 4915204
  114.6 7.4 %collective-permute-start.21 = (bf16[144,768]{1,0:T(8,128)(2,1)S(1)}, bf16[144,768]{1,0:T(8,128)(2,1)S(1)}, u32[]{:S(2)}, u32[]{:S(2)}) collective-permute-start(bf16[144,768]{1,0:T(8,128)(2,1)S(1)} %get-tuple-element.52), channel_id=1, source_target_pairs={{0,6},{2,0},{4,2},{6,4},{1,7},{3,1},{5,3},{7,5},{8,14},{10,8},{12,... | collective-permute-start | bytes 663560 | tf_op jit(solution)/shard_map/ppermute | solution.py:21
  116.8 6.4 %collective-permute-start.22 = (bf16[144,768]{1,0:T(8,128)(2,1)S(1)}, bf16[144,768]{1,0:T(8,128)(2,1)S(1)}, u32[]{:S(2)}, u32[]{:S(2)}) collective-permute-start(bf16[144,768]{1,0:T(8,128)(2,1)S(1)} %get-tuple-element.53), channel_id=1, source_target_pairs={{0,4},{2,6},{4,0},{6,2},{1,5},{3,7},{5,1},{7,3},{8,12},{10,14},{12... | collective-permute-start | bytes 663560 | tf_op jit(solution)/shard_map/ppermute | solution.py:21
  117.5 7.9 %collective-permute-start.23 = (bf16[144,768]{1,0:T(8,128)(2,1)S(1)}, bf16[144,768]{1,0:T(8,128)(2,1)S(1)}, u32[]{:S(2)}, u32[]{:S(2)}) collective-permute-start(bf16[144,768]{1,0:T(8,128)(2,1)S(1)} %get-tuple-element.54), channel_id=1, source_target_pairs={{0,2},{2,4},{4,6},{6,0},{1,3},{3,5},{5,7},{7,1},{8,10},{10,12},{12... | collective-permute-start | bytes 663560 | tf_op jit(solution)/shard_map/ppermute | solution.py:21
  127.1 11.8 %collective-permute-start.24 = (bf16[72,1280]{1,0:T(8,128)(2,1)S(1)}, bf16[72,1280]{1,0:T(8,128)(2,1)S(1)}, u32[]{:S(2)}, u32[]{:S(2)}) collective-permute-start(bf16[72,1280]{1,0:T(8,128)(2,1)S(1)} %dynamic-slice_bitcast_fusion), channel_id=1, source_target_pairs={{0,1},{1,0},{2,3},{3,2},{4,5},{5,4},{6,7},{7,6},{8,9},{9,8},{10,11... | collective-permute-start | bytes 552968 | tf_op jit(solution)/shard_map/ppermute | solution.py:21
